TPU v7x, 256 devices: a whole 4x4x8 slice. The times are simulated.
256 devices in a mesh: dp: 2 (over y_hi), tm: 32 (over z, y_lo, core), rows: 4 (over x).
Axes of the slice: x: 4, y: 4 (y_hi: 2, y_lo: 2; y = y_hi * 2 + y_lo), z: 8, core: 2. Of those that a mesh axis runs over, the one named last changes fastest.
Arguments:
- clips: bfloat16 [2, 64, 4, 128, 256], P('dp', 'tm', 'rows'), may hold values from -12 to 12
- weight: bfloat16 [3, 3, 3, 256, 256], replicated, may hold values from -0.078125 to 0.078125
- bias: float32 [256], replicated, may hold values from -1 to 1
- head: float32 [256], replicated, may hold values from -4 to 4
Outputs:
- grad_weight: float32 [3, 3, 3, 256, 256], replicated
- grad_bias: float32 [256], replicated
- grad_head: float32 [256], replicated
All inputs are finite; a program needn't handle non-finite values.
Results may differ from a plain program's by a relative error of at most 0.0003.
Values may be sent and summed in bfloat16 or wider, within the bound.
A program may use at most 128 MiB of HBM per device.

v0:
```python
import jax
import jax.numpy as jnp
from jax import lax
from jax.sharding import PartitionSpec as P

penalty_weight = 0.01


def padded_2(value, sides, width):
    for axis, dim in sides:
        count, length = (lax.axis_size(axis), value.shape[dim])
        up = [(i, (i + 1) % count) for i in range(count - 1)]
        down = [(j, i) for i, j in up]
        last = lax.slice_in_dim(value, length - width, length, axis=dim)
        initial = lax.slice_in_dim(value, 0, width, axis=dim)
        before = lax.ppermute(last, axis, up)
        after = lax.ppermute(initial, axis, down)
        value = jnp.concatenate([before, value, after], axis=dim)
    return value


def conv_offsets(padded, weight, transpose):
    nclip, tpad, rpad, wpad, chans = padded.shape
    frames, rowsn, cols = (tpad - 2, rpad - 2, wpad - 2)
    total = jnp.zeros((nclip * frames * rowsn * cols, weight.shape[4]), jnp.float32)
    for a in range(3):
        for b in range(3):
            for d in range(3):
                if transpose:
                    piece = padded[
                        :, 2 - a : 2 - a + frames, 2 - b : 2 - b + rowsn, 2 - d : 2 - d + cols
                    ]
                    total = total + lax.dot_general(
                        piece.reshape(-1, chans),
                        weight[a, b, d],
                        (((1,), (1,)), ((), ())),
                        preferred_element_type=jnp.float32,
                    )
                else:
                    piece = padded[:, a : a + frames, b : b + rowsn, d : d + cols]
                    total = total + jnp.dot(
                        piece.reshape(-1, chans),
                        weight[a, b, d],
                        preferred_element_type=jnp.float32,
                    )
    return total.reshape(nclip, frames, rowsn, cols, -1)


def correlate(padded, right):
    nclip, tpad, rpad, wpad, chans = padded.shape
    frames, rowsn, cols = (tpad - 2, rpad - 2, wpad - 2)
    right_rows = right.reshape(-1, right.shape[-1])
    blocks = []
    for a in range(3):
        for b in range(3):
            for d in range(3):
                piece = padded[:, a : a + frames, b : b + rowsn, d : d + cols].reshape(-1, chans)
                blocks.append(
                    lax.dot_general(
                        piece,
                        right_rows,
                        (((0,), (0,)), ((), ())),
                        preferred_element_type=jnp.float32,
                    )
                )
    return jnp.stack(blocks).reshape(3, 3, 3, chans, right.shape[-1])


def pad_columns(field):
    return jnp.pad(field, ((0, 0), (0, 0), (0, 0), (1, 1), (0, 0)))


def per_device(clips, weight, bias, head):
    clip_pad = pad_columns(padded_2(clips, (("tm", 1), ("rows", 2)), 1))
    pre = conv_offsets(clip_pad, weight, False) + bias
    sig = jax.nn.sigmoid(pre)
    slope = sig * (1.0 + pre * (1.0 - sig))
    curve = sig * (1.0 - sig) * (2.0 + pre * (1.0 - 2.0 * sig))
    score_grad = (head * slope).astype(jnp.bfloat16)
    score_pad = pad_columns(padded_2(score_grad, (("tm", 1), ("rows", 2)), 1))
    input_grad = conv_offsets(score_pad, weight, True).astype(jnp.bfloat16)
    grad_pad = pad_columns(padded_2(input_grad, (("tm", 1), ("rows", 2)), 1))
    back_grad = penalty_weight * conv_offsets(grad_pad, weight, False)
    pre_grad = back_grad * head * curve
    pre_grad_b = pre_grad.astype(jnp.bfloat16)
    local_weight = penalty_weight * correlate(grad_pad, score_grad) + correlate(
        clip_pad, pre_grad_b
    )
    local_bias = jnp.sum(pre_grad, axis=(0, 1, 2, 3))
    local_head = jnp.sum(back_grad * slope, axis=(0, 1, 2, 3))
    grad_weight, grad_bias, grad_head = lax.psum(
        (local_weight, local_bias, local_head), ("dp", "tm", "rows")
    )
    return (grad_weight, grad_bias, grad_head)


def solution(mesh):
    return jax.shard_map(
        per_device,
        mesh=mesh,
        in_specs=(P("dp", "tm", "rows", None, None), P(), P(), P()),
        out_specs=(P(), P(), P()),
        check_vma=False,
    )
```

profile of v0, /device:TPU:1, one launch (start us, length us, event | category | flops | bytes accessed | tf_op | source)
XLA Modules:
  0.0 534.8 jit_solution(14304096221612865775)
XLA Ops:
  8.3 4.6 collective-permute-start
  12.8 1.9 collective-permute-start.1
  14.8 3.6 collective-permute-done.1
  18.5 3.1 collective-permute-start.2
  25.7 4.1 collective-permute-done.3
  33.3 2.0 fusion.385
  101.1 3.4 collective-permute-start.4
  104.5 1.9 collective-permute-start.5
  106.4 3.6 collective-permute-done.5
  110.1 3.1 collective-permute-start.6
  114.6 2.8 collective-permute-done.6
  117.4 4.1 collective-permute-done.7
  128.5 3.5 collective-permute-start.8
  132.0 1.9 collective-permute-start.9
  133.9 4.3 collective-permute-done.9
  138.3 2.8 collective-permute-start.10
  144.6 4.1 collective-permute-done.11
  150.3 2.0 fusion.384
  157.9 3.0 copy-done.5
  178.2 1.9 fusion.217
  237.8 4.1 multiply_add_fusion
  241.9 82.1 %all-reduce.3 = (f32[256]{0:T(256)}, f32[256]{0:T(256)}) all-reduce(f32[256]{0:T(256)S(1)} %get-tuple-element.5, f32[256]{0:T(256)S(1)} %get-tuple-element.61), channel_id=1, replica_groups=mesh['dp'=2,'tm'=32,'rows'=4] {'dp','tm','rows'}, use_global_device_ids=true, to_apply=%region_2.3 | all-reduce | flops 512 | bytes 4096 | tf_op jit(solution)/shard_map/psum | solution.py:91
  324.0 197.2 %all-reduce.6.cloned.1.call-done = f32[3,3,3,256,256]{4,3,2,1,0:T(8,128)} async-done(((f32[3,3,3,256,256]{4,3,2,1,0:T(8,128)}), f32[3,3,3,256,256]{4,3,2,1,0:T(8,128)}) %all-reduce.6.cloned.1.call-update) | async-done | bytes 7077904 | tf_op jit(solution)/shard_map/psum | solution.py:91
  521.2 6.7 %copy.139 = f32[3,3,3,256,256]{4,3,2,1,0:T(8,128)} copy(f32[3,3,3,256,256]{4,3,2,1,0:T(8,128)} %all-reduce.6.cloned.1.call-done) | data formatting | bytes 14155776
  (335 shorter events, 167.0 us)
Async XLA Ops:
  7.2 514.0 %all-reduce.6.cloned.1.call-start = ((), (), s32[]{:S(2)}) async-start(), calls=%async_computation | async-start | bytes 14155776 | tf_op jit(solution)/shard_map/psum | solution.py:91
  8.3 6.5 %collective-permute-start = (bf16[1,1,1,128,256]{3,4,1,2,0:T(8,128)(2,1)S(1)}, bf16[1,1,1,128,256]{3,4,1,2,0:T(8,128)(2,1)S(1)}, u32[]{:S(2)}, u32[]{:S(2)}) collective-permute-start(bf16[1,1,1,128,256]{3,4,1,2,0:T(8,128)(2,1)S(1)} %get-tuple-element.90), channel_id=1, source_target_pairs={{0,4},{4,8},{8,12},{12,16},{16,20},{20,24},{24,28},{28,32},{32,36}... | collective-permute-start | bytes 196616 | tf_op jit(solution)/shard_map/ppermute | solution.py:16
  12.8 5.6 %collective-permute-start.1 = (bf16[1,1,1,128,256]{3,4,1,2,0:T(8,128)(2,1)S(1)}, bf16[1,1,1,128,256]{3,4,1,2,0:T(8,128)(2,1)S(1)}, u32[]{:S(2)}, u32[]{:S(2)}) collective-permute-start(bf16[1,1,1,128,256]{3,4,1,2,0:T(8,128)(2,1)S(1)} %get-tuple-element.91), channel_id=1, source_target_pairs={{4,0},{8,4},{12,8},{16,12},{20,16},{24,20},{28,24},{32,28},{36,32}... | collective-permute-start | bytes 196616 | tf_op jit(solution)/shard_map/ppermute | solution.py:17
  18.5 7.3 %collective-permute-start.2 = (bf16[1,4,1,128,256]{3,4,1,2,0:T(8,128)(2,1)S(1)}, bf16[1,4,1,128,256]{3,4,1,2,0:T(8,128)(2,1)S(1)}, u32[]{:S(2)}, u32[]{:S(2)}) collective-permute-start(bf16[1,4,1,128,256]{3,4,1,2,0:T(8,128)(2,1)S(1)} %pad_maximum_fusion), channel_id=1, source_target_pairs={{0,1},{1,2},{2,3},{4,5},{5,6},{6,7},{8,9},{9,10},{10,11},{12,13},{... | collective-permute-start | bytes 786440 | tf_op jit(solution)/shard_map/ppermute | solution.py:16
  21.6 8.2 %collective-permute-start.3 = (bf16[1,4,1,128,256]{3,4,1,2,0:T(8,128)(2,1)S(1)}, bf16[1,4,1,128,256]{3,4,1,2,0:T(8,128)(2,1)S(1)}, u32[]{:S(2)}, u32[]{:S(2)}) collective-permute-start(bf16[1,4,1,128,256]{3,4,1,2,0:T(8,128)(2,1)S(1)} %pad_maximum_fusion), channel_id=1, source_target_pairs={{1,0},{2,1},{3,2},{5,4},{6,5},{7,6},{9,8},{10,9},{11,10},{13,12},{... | collective-permute-start | bytes 786440 | tf_op jit(solution)/shard_map/ppermute | solution.py:17
  22.9 6.9 %copy-start.16 = (bf16[1,2,1,128,256]{3,4,1,2,0:T(8,128)(2,1)}, bf16[1,2,1,128,256]{3,4,1,2,0:T(8,128)(2,1)S(1)}, u32[]{:S(2)}) copy-start(bf16[1,2,1,128,256]{3,4,1,2,0:T(8,128)(2,1)S(1)} %get-tuple-element.88) | copy-start | bytes 393220
  23.0 6.9 %copy-start.18 = (bf16[1,2,1,128,256]{3,4,1,2,0:T(8,128)(2,1)}, bf16[1,2,1,128,256]{3,4,1,2,0:T(8,128)(2,1)S(1)}, u32[]{:S(2)}) copy-start(bf16[1,2,1,128,256]{3,4,1,2,0:T(8,128)(2,1)S(1)} %get-tuple-element.89) | copy-start | bytes 393220
  33.3 8.8 %copy-start = (bf16[3,3,3,256,256]{4,3,2,1,0:T(8,128)(2,1)S(1)}, bf16[3,3,3,256,256]{4,3,2,1,0:T(8,128)(2,1)}, u32[]{:S(2)}) copy-start(bf16[3,3,3,256,256]{4,3,2,1,0:T(8,128)(2,1)} %param.5) | copy-start | bytes 10616836
  91.3 6.7 %copy-start.36 = (bf16[1,2,1,128,256]{4,3,1,2,0:T(8,128)(2,1)S(1)}, bf16[1,2,1,128,256]{4,3,1,2,0:T(8,128)(2,1)}, u32[]{:S(2)}) copy-start(bf16[1,2,1,128,256]{4,3,1,2,0:T(8,128)(2,1)} %copy.35) | copy-start | bytes 393220
  101.1 5.3 collective-permute-start.4
  104.5 5.6 %collective-permute-start.5 = (bf16[1,1,1,128,256]{4,3,1,2,0:T(8,128)(2,1)S(1)}, bf16[1,1,1,128,256]{4,3,1,2,0:T(8,128)(2,1)S(1)}, u32[]{:S(2)}, u32[]{:S(2)}) collective-permute-start(bf16[1,1,1,128,256]{4,3,1,2,0:T(8,128)(2,1)S(1)} %get-tuple-element.87), channel_id=1, source_target_pairs={{4,0},{8,4},{12,8},{16,12},{20,16},{24,20},{28,24},{32,28},{36,32}... | collective-permute-start | bytes 196616 | tf_op jit(solution)/shard_map/ppermute | solution.py:17
  110.1 7.3 %collective-permute-start.6 = (bf16[1,4,1,128,256]{4,3,1,2,0:T(8,128)(2,1)S(1)}, bf16[1,4,1,128,256]{4,3,1,2,0:T(8,128)(2,1)S(1)}, u32[]{:S(2)}, u32[]{:S(2)}) collective-permute-start(bf16[1,4,1,128,256]{4,3,1,2,0:T(8,128)(2,1)S(1)} %pad_maximum_fusion.1), channel_id=1, source_target_pairs={{0,1},{1,2},{2,3},{4,5},{5,6},{6,7},{8,9},{9,10},{10,11},{12,13},{... | collective-permute-start | bytes 786440 | tf_op jit(solution)/shard_map/ppermute | solution.py:16
  113.3 8.2 %collective-permute-start.7 = (bf16[1,4,1,128,256]{4,3,1,2,0:T(8,128)(2,1)S(1)}, bf16[1,4,1,128,256]{4,3,1,2,0:T(8,128)(2,1)S(1)}, u32[]{:S(2)}, u32[]{:S(2)}) collective-permute-start(bf16[1,4,1,128,256]{4,3,1,2,0:T(8,128)(2,1)S(1)} %pad_maximum_fusion.1), channel_id=1, source_target_pairs={{1,0},{2,1},{3,2},{5,4},{6,5},{7,6},{9,8},{10,9},{11,10},{13,12},{... | collective-permute-start | bytes 786440 | tf_op jit(solution)/shard_map/ppermute | solution.py:17
  128.3 26.6 %copy-start.12 = (bf16[256,256]{1,0:T(8,128)(2,1)}, bf16[256,256]{1,0:T(8,128)(2,1)S(1)}, u32[]{:S(2)}) copy-start(bf16[256,256]{1,0:T(8,128)(2,1)S(1)} %fusion.87) | copy-start | bytes 393220
  128.5 5.4 %collective-permute-start.8 = (bf16[1,1,1,128,256]{3,4,1,2,0:T(8,128)(2,1)S(1)}, bf16[1,1,1,128,256]{3,4,1,2,0:T(8,128)(2,1)S(1)}, u32[]{:S(2)}, u32[]{:S(2)}) collective-permute-start(bf16[1,1,1,128,256]{3,4,1,2,0:T(8,128)(2,1)S(1)} %get-tuple-element.82), channel_id=1, source_target_pairs={{0,4},{4,8},{8,12},{12,16},{16,20},{20,24},{24,28},{28,32},{32,36}... | collective-permute-start | bytes 196616 | tf_op jit(solution)/shard_map/ppermute | solution.py:16
  132.0 6.3 %collective-permute-start.9 = (bf16[1,1,1,128,256]{3,4,1,2,0:T(8,128)(2,1)S(1)}, bf16[1,1,1,128,256]{3,4,1,2,0:T(8,128)(2,1)S(1)}, u32[]{:S(2)}, u32[]{:S(2)}) collective-permute-start(bf16[1,1,1,128,256]{3,4,1,2,0:T(8,128)(2,1)S(1)} %get-tuple-element.83), channel_id=1, source_target_pairs={{4,0},{8,4},{12,8},{16,12},{20,16},{24,20},{28,24},{32,28},{36,32}... | collective-permute-start | bytes 196616 | tf_op jit(solution)/shard_map/ppermute | solution.py:17
  138.3 6.3 %collective-permute-start.10 = (bf16[1,4,1,128,256]{3,4,1,2,0:T(8,128)(2,1)S(1)}, bf16[1,4,1,128,256]{3,4,1,2,0:T(8,128)(2,1)S(1)}, u32[]{:S(2)}, u32[]{:S(2)}) collective-permute-start(bf16[1,4,1,128,256]{3,4,1,2,0:T(8,128)(2,1)S(1)} %pad_maximum_fusion.2), channel_id=1, source_target_pairs={{0,1},{1,2},{2,3},{4,5},{5,6},{6,7},{8,9},{9,10},{10,11},{12,13},{... | collective-permute-start | bytes 786440 | tf_op jit(solution)/shard_map/ppermute | solution.py:16
  141.1 7.6 %collective-permute-start.11 = (bf16[1,4,1,128,256]{3,4,1,2,0:T(8,128)(2,1)S(1)}, bf16[1,4,1,128,256]{3,4,1,2,0:T(8,128)(2,1)S(1)}, u32[]{:S(2)}, u32[]{:S(2)}) collective-permute-start(bf16[1,4,1,128,256]{3,4,1,2,0:T(8,128)(2,1)S(1)} %pad_maximum_fusion.2), channel_id=1, source_target_pairs={{1,0},{2,1},{3,2},{5,4},{6,5},{7,6},{9,8},{10,9},{11,10},{13,12},{... | collective-permute-start | bytes 786440 | tf_op jit(solution)/shard_map/ppermute | solution.py:17
  144.6 11.7 %copy-start.11 = (bf16[1,4,1,128,256]{3,4,1,2,0:T(8,128)(2,1)}, bf16[1,4,1,128,256]{3,4,1,2,0:T(8,128)(2,1)S(1)}, u32[]{:S(2)}) copy-start(bf16[1,4,1,128,256]{3,4,1,2,0:T(8,128)(2,1)S(1)} %collective-permute-done.10) | copy-start | bytes 786436
  148.7 8.8 %copy-start.10 = (bf16[1,4,1,128,256]{3,4,1,2,0:T(8,128)(2,1)}, bf16[1,4,1,128,256]{3,4,1,2,0:T(8,128)(2,1)S(1)}, u32[]{:S(2)}) copy-start(bf16[1,4,1,128,256]{3,4,1,2,0:T(8,128)(2,1)S(1)} %collective-permute-done.11) | copy-start | bytes 786436
  160.9 31.1 %copy-start.2 = (bf16[3,3,3,256,256]{4,3,2,1,0:T(8,128)(2,1)S(1)}, bf16[3,3,3,256,256]{4,3,2,1,0:T(8,128)(2,1)}, u32[]{:S(2)}) copy-start(bf16[3,3,3,256,256]{4,3,2,1,0:T(8,128)(2,1)} %param.5) | copy-start | bytes 10616836
  192.0 6.5 %copy-start.41 = (bf16[1,2,1,128,256]{4,3,1,2,0:T(8,128)(2,1)S(1)}, bf16[1,2,1,128,256]{4,3,1,2,0:T(8,128)(2,1)}, u32[]{:S(2)}) copy-start(bf16[1,2,1,128,256]{4,3,1,2,0:T(8,128)(2,1)} %copy.67) | copy-start | bytes 393220
  224.9 6.5 %copy-start.38 = (bf16[1,2,1,128,256]{4,3,1,2,0:T(8,128)(2,1)S(1)}, bf16[1,2,1,128,256]{4,3,1,2,0:T(8,128)(2,1)}, u32[]{:S(2)}) copy-start(bf16[1,2,1,128,256]{4,3,1,2,0:T(8,128)(2,1)} %copy.77) | copy-start | bytes 393220
  224.9 6.7 %copy-start.37 = (bf16[1,2,1,128,256]{4,3,1,2,0:T(8,128)(2,1)S(1)}, bf16[1,2,1,128,256]{4,3,1,2,0:T(8,128)(2,1)}, u32[]{:S(2)}) copy-start(bf16[1,2,1,128,256]{4,3,1,2,0:T(8,128)(2,1)} %copy.78) | copy-start | bytes 393220
  (47 other events, 181.1 us)
Sparse Core Ops, SparseCore 0:
  242.1 279.1 all-reduce.5
where the time goes:
time: 538 us; the launch traced here: 535 us
  waiting for transfers between devices  226 us (42%)
  local copies, waits for them, and re-layouts  108 us (20%)
  blocking collectives  82.1 us (15%)
  matrix products  65.3 us (12%)
  starting transfers between devices  30.4 us (6%)
  between operations  15.9 us (3%)
  other arithmetic  7.71 us (1%)
    psum x1, waiting for transfers between devices, per_device(): lax.psum((local_weight, local_bias, local_head), ('dp', 'tm', 'rows'))  197 us
    psum x1, blocking collectives, per_device(): lax.psum((local_weight, local_bias, local_head), ('dp', 'tm', 'rows'))  82.1 us
    dot_general x54, matrix products, conv_offsets(): jnp.dot(piece.reshape(-1, chans), weight[a, b, d], preferred_element_type...  48.5 us
    slice x29, local copies, waits for them, and re-layouts, correlate(): piece = padded[:, a:a + frames, b:b + rowsn, d:d + cols].reshape(-1, chans)  47.1 us
    slice x29, local copies, waits for them, and re-layouts, conv_offsets(): piece = padded[:, a:a + frames, b:b + rowsn, d:d + cols]  46.9 us
    ppermute x6, waiting for transfers between devices, padded_2(): after = lax.ppermute(initial, axis, down)  23.9 us
    ppermute x6, starting transfers between devices, padded_2(): before = lax.ppermute(last, axis, up)  20.6 us
    unnamed x118, local copies, waits for them, and re-layouts  13.2 us
  transfers between devices with their start and end apart: 13, of which 10 were waited for; matrix products, arithmetic and copies ran while one was open for 1% of the time, Pallas kernels for 0%

commit v1 on v0

v1 whole, which is shorter than its diff:
```python
import functools

import jax
import jax.numpy as jnp
from jax import lax
from jax.experimental import pallas as pl
from jax.experimental.pallas import tpu as pltpu
from jax.sharding import PartitionSpec as P

MESH = pl.DeviceIdType.MESH
F32 = jnp.float32
BF16 = jnp.bfloat16
penalty_weight = 0.01
C = 256
NTM = 32
NREMOTE = 112


def kernel(
    clips_ref, w_hbm, bias_ref, head_ref, gw_hbm, small_ref,
    wv, wt, slabs, xraw, xcat, sraw, shl, shr, scat, graw, ghl, ghr, gcat,
    scells, gcells, vals, acc, slope_s, curve_s, sg_s, pgb_s,
    gh, oh, rc, ra, rb, rz, r2a, r2b, r2c, r3z, r3y,
    wsem, osem, send_sems, recv_sems,
):
    dp = lax.axis_index("dp")
    tm = lax.axis_index("tm")
    x = lax.axis_index("rows")
    core = lax.rem(tm, 2)
    y = dp * 2 + lax.rem(tm // 2, 2)
    z = tm // 4
    has_prev = tm > 0
    has_next = tm < NTM - 1
    has_left = x > 0
    has_right = x < 3

    def dev(xx, yy, zz, cc):
        return (yy // 2, zz * 4 + lax.rem(yy, 2) * 2 + cc, xx)

    def xp(s):
        return lax.rem(x + s, 4)

    def yp(s):
        return lax.rem(y + s, 4)

    def zp(s):
        return lax.rem(z + s, 8)

    other = 1 - core
    partner = dev(x, y, z, other)

    counter = [0]
    sends = []

    def remote(src, dst, target):
        n = counter[0]
        counter[0] += 1
        return pltpu.make_async_remote_copy(
            src_ref=src, dst_ref=dst, send_sem=send_sems.at[n], recv_sem=recv_sems.at[n],
            device_id=target, device_id_type=MESH,
        )

    wcopy = pltpu.make_async_copy(w_hbm, wv, wsem)
    wcopy.start()

    barrier = pltpu.get_barrier_semaphore()

    def greet(target):
        pl.semaphore_signal(barrier, inc=1, device_id=target, device_id_type=MESH)

    greet(partner)
    for s in range(1, 4):
        greet(dev(xp(s), y, z, core))
        greet(dev(x, yp(s), z, core))
    for s in range(1, 8):
        greet(dev(x, y, zp(s), core))

    @pl.when(has_prev)
    def _():
        for s in range(4):
            greet((dp, tm - 1, xp(s)))

    @pl.when(has_next)
    def _():
        for s in range(4):
            greet((dp, tm + 1, xp(s)))

    for f in range(2):
        v = clips_ref[f].astype(F32)
        edge = jnp.zeros((8, C), F32)
        v = jnp.concatenate([edge, v, edge], axis=0)
        for c in range(4):
            slabs[c, f] = v[32 * c:32 * c + 48].astype(BF16)
    xraw[1, x] = slabs[x, 0]
    xraw[2, x] = slabs[x, 1]
    zrow = jnp.zeros((4, 32, 768), BF16)
    for cat in (xcat, scat, gcat):
        cat[:, 0] = zrow
        cat[:, 5] = zrow

    @pl.when(jnp.logical_not(has_prev))
    def _():
        xraw[0] = jnp.zeros((4, 48, C), BF16)
        for raw, hl, hr in ((sraw, shl, shr), (graw, ghl, ghr)):
            raw[0] = jnp.zeros((4, 32, C), BF16)
            hl[0] = jnp.zeros((8, C), F32)
            hr[0] = jnp.zeros((8, C), F32)

    @pl.when(jnp.logical_not(has_next))
    def _():
        xraw[3] = jnp.zeros((4, 48, C), BF16)
        for raw, hl, hr in ((sraw, shl, shr), (graw, ghl, ghr)):
            raw[3] = jnp.zeros((4, 32, C), BF16)
            hl[3] = jnp.zeros((8, C), F32)
            hr[3] = jnp.zeros((8, C), F32)

    @pl.when(jnp.logical_not(has_left))
    def _():
        for hl in (shl, ghl):
            hl[...] = jnp.zeros((4, 8, C), F32)

    @pl.when(jnp.logical_not(has_right))
    def _():
        for hr in (shr, ghr):
            hr[...] = jnp.zeros((4, 8, C), F32)

    for cells in (scells, gcells):
        cells[...] = jnp.zeros((2, 2, 8, C), F32)

    pl.semaphore_wait(
        barrier, 14 + 4 * has_prev.astype(jnp.int32) + 4 * has_next.astype(jnp.int32)
    )

    same = [remote(slabs.at[xp(s)], xraw.at[pl.ds(1, 2), x], (dp, tm, xp(s))) for s in range(1, 4)]
    nxt = [remote(slabs.at[xp(s), 1], xraw.at[0, x], (dp, tm + 1, xp(s))) for s in range(4)]
    prv = [remote(slabs.at[xp(s), 0], xraw.at[3, x], (dp, tm - 1, xp(s))) for s in range(4)]

    def exchange(groups):
        for can_send, _, copies in groups:
            @pl.when(can_send)
            def _():
                for copy in copies:
                    copy.start()
        sends.extend((can_send, copies) for can_send, _, copies in groups)

    def arrive(groups):
        for _, can_receive, copies in groups:
            @pl.when(can_receive)
            def _():
                for copy in copies:
                    copy.wait_recv()

    always = tm >= 0
    first = ((always, always, same), (has_next, has_prev, nxt), (has_prev, has_next, prv))
    exchange(first)
    wcopy.wait()
    for k in range(9):
        a, b = k // 3, k % 3
        for d in range(3):
            src = wv[(2 - a) * 3 + 2 - b, (2 - d) * 256:(3 - d) * 256]
            wt[k, d * 256:(d + 1) * 256] = src.T
    arrive(first)

    def first_cat(n, _):
        f, r = n // 4, lax.rem(n, 4)
        v = xraw[f, r].astype(F32)
        for d in range(3):
            xcat[f, r + 1, :, d * C:(d + 1) * C] = v[7 + d:39 + d].astype(BF16)
        return 0

    lax.fori_loop(0, 16, first_cat, 0)

    def conv(cat, weights):
        acc[...] = jnp.zeros((256, C), F32)

        def body(k, _):
            a, b = k // 3, lax.rem(k, 3)
            lhs = cat[pl.ds(a, 2), pl.ds(b, 4)].reshape(256, 768)
            acc[...] += jnp.dot(lhs, weights[k], preferred_element_type=F32)
            return 0

        lax.fori_loop(0, 9, body, 0)
        return acc[...]

    def halo(value, raw, hl, hr, cells):
        raw[1:3] = value.reshape(2, 4, 32, C)
        vals[...] = value.astype(F32).reshape(2, 4, 32, C)
        for f in range(2):
            for r in range(4):
                cells[0, f, r:r + 1] = vals[f, r, 0:1]
                cells[1, f, r:r + 1] = vals[f, r, 31:32]
        first_cells, last_cells = cells.at[0], cells.at[1]
        groups = (
            (has_next, has_prev, [remote(raw.at[2], raw.at[0], (dp, tm + 1, x))]),
            (has_prev, has_next, [remote(raw.at[1], raw.at[3], (dp, tm - 1, x))]),
            (has_right, has_left, [remote(last_cells, hl.at[pl.ds(1, 2)], (dp, tm, x + 1))]),
            (has_left, has_right, [remote(first_cells, hr.at[pl.ds(1, 2)], (dp, tm, x - 1))]),
            (has_next & has_right, has_prev & has_left, [remote(last_cells.at[1], hl.at[0], (dp, tm + 1, x + 1))]),
            (has_next & has_left, has_prev & has_right, [remote(first_cells.at[1], hr.at[0], (dp, tm + 1, x - 1))]),
            (has_prev & has_right, has_next & has_left, [remote(last_cells.at[0], hl.at[3], (dp, tm - 1, x + 1))]),
            (has_prev & has_left, has_next & has_right, [remote(first_cells.at[0], hr.at[3], (dp, tm - 1, x - 1))]),
        )
        exchange(groups)
        return groups

    def make_cat(raw, hl, hr, cat):
        def body(n, _):
            f, r = n // 4, lax.rem(n, 4)
            b = raw[f, r]
            v = b.astype(F32)
            row = lax.broadcasted_iota(jnp.int32, (32, C), 0)
            low = hl[f, pl.ds(r, 1)]
            high = hr[f, pl.ds(r, 1)]
            cat[f, r + 1, :, 0:C] = jnp.where(row == 0, low, pltpu.roll(v, 1, 0)).astype(BF16)
            cat[f, r + 1, :, C:2 * C] = b
            cat[f, r + 1, :, 2 * C:3 * C] = jnp.where(row == 31, high, pltpu.roll(v, 31, 0)).astype(BF16)
            return 0

        lax.fori_loop(0, 16, body, 0)

    pre = conv(xcat, wv) + bias_ref[...]
    sig = jax.nn.sigmoid(pre)
    slope = sig * (1.0 + pre * (1.0 - sig))
    slope_s[...] = slope
    curve_s[...] = sig * (1.0 - sig) * (2.0 + pre * (1.0 - 2.0 * sig))
    sg = (head_ref[...] * slope).astype(BF16)
    sg_s[...] = sg
    groups = halo(sg, sraw, shl, shr, scells)
    arrive(groups)
    make_cat(sraw, shl, shr, scat)
    ig = conv(scat, wt).astype(BF16)
    groups = halo(ig, graw, ghl, ghr, gcells)
    arrive(groups)
    make_cat(graw, ghl, ghr, gcat)
    back = penalty_weight * conv(gcat, wv)
    pre_grad = back * head_ref[...] * curve_s[...]
    pgb_s[...] = pre_grad.astype(BF16)
    bias_row = jnp.sum(pre_grad, axis=0, keepdims=True)
    head_row = jnp.sum(back * slope_s[...], axis=0, keepdims=True)

    def correlate(k, _):
        a, b = k // 3, lax.rem(k, 3)
        dims = (((0,), (0,)), ((), ()))
        g = gcat[pl.ds(a, 2), pl.ds(b, 4)].reshape(256, 768)
        total = penalty_weight * lax.dot_general(g, sg_s[...], dims, preferred_element_type=F32)
        g = xcat[pl.ds(a, 2), pl.ds(b, 4)].reshape(256, 768)
        total += lax.dot_general(g, pgb_s[...], dims, preferred_element_type=F32)
        for d in range(3):
            tap = 3 * k + d
            for h in range(2):
                gh[h, tap // 4, lax.rem(tap, 4)] = total[
                    d * 256:(d + 1) * 256, h * 128:(h + 1) * 128
                ].reshape(4, 8, 8, 128)
        return 0

    spans = ((0, 3), (3, 3), (6, 1))
    zero = []
    for n, (lo, hi) in enumerate(((0, 4), (4, 8), (8, 9))):
        lax.fori_loop(lo, hi, correlate, 0)
        if n == 2:
            tile = lax.broadcasted_iota(jnp.int32, (8, 128), 0)
            for h in range(2):
                gh[h, 6, 3] = jnp.zeros((4, 8, 8, 128), F32)
                gh[h, 6, 3, 0, 0] = jnp.where(
                    tile == 0, bias_row[:, h * 128:(h + 1) * 128],
                    jnp.where(tile == 1, head_row[:, h * 128:(h + 1) * 128], 0.0),
                )
        span = pl.ds(*spans[n])
        copy = remote(gh.at[other, span], rc.at[span], partner)
        copy.start()
        sends.append((always, [copy]))
        zero.append(copy)

    def launch(copies):
        for copy in copies:
            copy.start()
        sends.append((always, copies))

    def landed(copies):
        for copy in copies:
            copy.wait_recv()

    def add_core(n):
        zero[n].wait_recv()

        def body(j, _):
            gh[core, j] += rc[j]
            return 0

        lax.fori_loop(spans[n][0], spans[n][0] + spans[n][1], body, 0)

    mine = gh.at[core]
    A, B = pl.ds(0, 3), pl.ds(3, 3)
    AB = pl.ds(0, 6)
    add_core(0)
    one_a = [remote(mine.at[A, xp(s)], ra.at[s - 1], dev(xp(s), y, z, core)) for s in range(1, 4)]
    launch(one_a)
    add_core(1)
    one_b = [remote(mine.at[B, :, yp(s)], rb.at[s - 1], dev(x, yp(s), z, core)) for s in range(1, 4)]
    launch(one_b)
    add_core(2)
    one_c = [remote(mine.at[6, :, :, zp(s)], rz.at[s - 1], dev(x, y, zp(s), core)) for s in range(1, 8)]
    launch(one_c)

    landed(one_c)
    t = gh[core, 6, :, :, z]
    for s in range(7):
        t += rz[s]
    gh[core, 6, :, :, z] = t
    two_c = [remote(mine.at[6, xp(s), :, z], r2c.at[s - 1], dev(xp(s), y, z, core)) for s in range(1, 4)]
    launch(two_c)
    landed(one_a)
    for j in range(3):
        gh[core, j, x] += ra[0, j] + ra[1, j] + ra[2, j]
    two_a = [remote(mine.at[A, x, yp(s)], r2a.at[s - 1], dev(x, yp(s), z, core)) for s in range(1, 4)]
    launch(two_a)
    landed(one_b)
    for j in range(3):
        gh[core, 3 + j, :, y] += rb[0, j] + rb[1, j] + rb[2, j]
    two_b = [remote(mine.at[B, xp(s), y], r2b.at[s - 1], dev(xp(s), y, z, core)) for s in range(1, 4)]
    launch(two_b)
    landed(two_c)
    gh[core, 6, x, :, z] += r2c[0] + r2c[1] + r2c[2]
    three_c = [remote(mine.at[6, x, yp(s), z], r3y.at[s - 1], dev(x, yp(s), z, core)) for s in range(1, 4)]
    launch(three_c)
    landed(two_a)
    gh[core, 0:3, x, y] += r2a[0] + r2a[1] + r2a[2]
    landed(two_b)
    gh[core, 3:6, x, y] += r2b[0] + r2b[1] + r2b[2]
    three_z = [remote(mine.at[AB, x, y, zp(s)], r3z.at[s - 1], dev(x, y, zp(s), core)) for s in range(1, 8)]
    launch(three_z)

    out = oh.at[core]
    landed(three_c)
    oh[core, 6, x, y, z] = gh[core, 6, x, y, z] + r3y[0] + r3y[1] + r3y[2]
    piece = out.at[6, x, y, z]
    g1c = [remote(piece, piece, dev(x, yp(s), z, core)) for s in range(1, 4)]
    launch(g1c)
    landed(three_z)
    t = gh[core, 0:6, x, y, z]
    for s in range(7):
        t += r3z[s]
    oh[core, 0:6, x, y, z] = t
    piece = out.at[AB, x, y, z]
    g1z = [remote(piece, piece, dev(x, y, zp(s), core)) for s in range(1, 8)]
    launch(g1z)
    landed(g1c)
    piece = out.at[6, x, :, z]
    g2c = [remote(piece, piece, dev(xp(s), y, z, core)) for s in range(1, 4)]
    launch(g2c)
    landed(g1z)
    piece_a = out.at[A, x, y]
    g2a = [remote(piece_a, piece_a, dev(x, yp(s), z, core)) for s in range(1, 4)]
    launch(g2a)
    piece_b = out.at[B, x, y]
    g2b = [remote(piece_b, piece_b, dev(xp(s), y, z, core)) for s in range(1, 4)]
    launch(g2b)
    landed(g2c)
    piece_c = out.at[6, :, :, z]
    g3c = [remote(piece_c, piece_c, dev(x, y, zp(s), core)) for s in range(1, 8)]
    launch(g3c)
    landed(g2a)
    piece_a = out.at[A, x]
    g3a = [remote(piece_a, piece_a, dev(xp(s), y, z, core)) for s in range(1, 4)]
    launch(g3a)
    landed(g2b)
    piece_b = out.at[B, :, y]
    g3b = [remote(piece_b, piece_b, dev(x, yp(s), z, core)) for s in range(1, 4)]
    launch(g3b)
    last = []

    def hand(n):
        span = pl.ds(*spans[n])
        copy = remote(out.at[span], out.at[span], partner)
        launch([copy])
        last.append(copy)

    landed(g3c)
    hand(2)
    landed(g3a)
    hand(0)
    landed(g3b)
    hand(1)
    landed(last)
    writes = []
    for h in range(2):
        small_ref[:, h * 128:(h + 1) * 128] = oh[h, 6, 3, 0, 0]
        for n, (lo, taps) in enumerate(((0, 24), (24, 3))):
            src = oh.at[h, pl.ds(0, 6)] if n == 0 else oh.at[h, 6, pl.ds(0, 3)]
            if n == 0:
                dst = gw_hbm.at[pl.ds(0, 6), :, :, :, :, pl.ds(h * 128, 128)]
            else:
                dst = gw_hbm.at[6, pl.ds(0, 3), :, :, :, pl.ds(h * 128, 128)]
            writes.append(pltpu.make_async_copy(src, dst, osem.at[2 * h + n]))
            writes[-1].start()
    for copy in writes:
        copy.wait()
    for can_send, copies in sends:
        @pl.when(can_send)
        def _():
            for copy in copies:
                copy.wait_send()


def per_device(clips, weight, bias, head):
    vm = pltpu.VMEM
    half = (7, 4, 4, 8, 8, 128)
    field = lambda w: vm((4, 4, w, C), BF16)
    cells = vm((4, 8, C), F32)
    cat = vm((4, 6, 32, 768), BF16)
    plane = vm((256, C), F32)
    scratch = [
        vm((9, 768, C), BF16), vm((9, 768, C), BF16), vm((4, 2, 48, C), BF16), field(48), cat,
        field(32), cells, cells, cat, field(32), cells, cells, cat,
        vm((2, 2, 8, C), F32), vm((2, 2, 8, C), F32), vm((2, 4, 32, C), F32), plane, plane, plane,
        vm((256, C), BF16), vm((256, C), BF16),
        vm((2, *half), F32), vm((2, *half), F32), vm(half, F32),
        vm((3, 3, 4, 8, 8, 128), F32), vm((3, 3, 4, 8, 8, 128), F32), vm((7, 4, 4, 8, 128), F32),
        vm((3, 3, 8, 8, 128), F32), vm((3, 3, 8, 8, 128), F32), vm((3, 4, 8, 128), F32),
        vm((7, 6, 8, 128), F32), vm((3, 8, 128), F32),
        pltpu.SemaphoreType.DMA, pltpu.SemaphoreType.DMA((4,)),
        pltpu.SemaphoreType.DMA((NREMOTE,)), pltpu.SemaphoreType.DMA((NREMOTE,)),
    ]
    inside = pl.BlockSpec(memory_space=pltpu.VMEM)
    outside = pl.BlockSpec(memory_space=pl.ANY)
    gw, small = pl.pallas_call(
        kernel,
        out_shape=(
            jax.ShapeDtypeStruct((7, 4, 4, 8, 8, C), F32),
            jax.ShapeDtypeStruct((8, C), F32),
        ),
        in_specs=[inside, outside, inside, inside],
        out_specs=(outside, inside),
        scratch_shapes=scratch,
        compiler_params=pltpu.CompilerParams(
            collective_id=0, has_side_effects=True, vmem_limit_bytes=60 * 1024 * 1024
        ),
        name="section",
    )(clips.reshape(2, 128, C), weight.reshape(9, 768, C), bias.reshape(1, C), head.reshape(1, C))
    grad_weight = gw.reshape(28, C, C)[:27].reshape(3, 3, 3, C, C)
    return grad_weight, small[0], small[1]


def solution(mesh):
    return jax.shard_map(
        per_device,
        mesh=mesh,
        in_specs=(P("dp", "tm", "rows", None, None), P(), P(), P()),
        out_specs=(P(), P(), P()),
        check_vma=False,
    )
```

time: 538 us -> 123 us (0.23)
  waiting for transfers between devices: 226 us -> 0 us
  Pallas kernels: 0 us -> 114 us
  local copies, waits for them, and re-layouts: 108 us -> 8.07 us
  blocking collectives: 82.1 us -> 0 us
  matrix products: 65.3 us -> 0 us
  starting transfers between devices: 30.4 us -> 0 us
  between operations: 15.9 us -> 0.64 us
  other arithmetic: 7.71 us -> 0 us
    psum x1 -> x0, waiting for transfers between devices: 197 us -> none  [per_device(): lax.psum((local_weight, local_bias, local_head), ('dp', 'tm', 'rows'))]
    pallas_call x0 -> x1, Pallas kernels: none -> 114 us  [per_device(): pl.pallas_call(kernel, out_shape=(jax.ShapeDtypeStruct((7, 4, 4, 8, 8, C)...]
    slice x64 -> x2, local copies, waits for them, and re-layouts: 94.5 us -> 8.07 us  [the longest x1 6.73 us: per_device(): grad_weight = gw.reshape(28, C, C)[:27].reshape(3, 3, 3, C, C)]
    psum x1 -> x0, blocking collectives: 82.1 us -> none  [per_device(): lax.psum((local_weight, local_bias, local_head), ('dp', 'tm', 'rows'))]
    dot_general x135 -> x0, matrix products: 65.3 us -> none  [the longest x54 48.5 us: conv_offsets(): jnp.dot(piece.reshape(-1, chans), weight[a, b, d], preferred_element_type...]
    ppermute x12 -> x0, starting transfers between devices: 30.4 us -> none  [the longest x6 20.6 us: padded_2(): before = lax.ppermute(last, axis, up)]
    ppermute x12 -> x0, waiting for transfers between devices: 28.4 us -> none  [the longest x6 23.9 us: padded_2(): after = lax.ppermute(initial, axis, down)]
    unnamed x118 -> x0, local copies, waits for them, and re-layouts: 13.2 us -> none
  transfers between devices with their start and end apart: 13 -> 0, of which waited for: 10 -> 0; matrix products, arithmetic and copies ran while one was open for 1% -> 0% of each run, Pallas kernels for 0% -> 0%
where the time goes in v1:
time: 123 us
  Pallas kernels  114 us (93%)
  local copies, waits for them, and re-layouts  8.07 us (7%)
    pallas_call x1, Pallas kernels, per_device(): pl.pallas_call(kernel, out_shape=(jax.ShapeDtypeStruct((7, 4, 4, 8, 8, C)...  114 us
    slice x1, local copies, waits for them, and re-layouts, per_device(): grad_weight = gw.reshape(28, C, C)[:27].reshape(3, 3, 3, C, C)  6.73 us

profile of v1, /device:TPU:1, one launch (start us, length us, event | category | flops | bytes accessed | tf_op | source)
XLA Modules:
  0.0 123.1 jit_solution(7565245273844300857)
XLA Ops:
  0.6 114.4 %section.1 = (f32[7,4,4,8,8,256]{5,4,3,2,1,0:T(8,128)}, f32[8,256]{1,0:T(8,128)}) custom-call(bf16[2,128,256]{2,1,0:T(8,128)(2,1)} %bitcast.11, bf16[9,768,256]{2,1,0:T(8,128)(2,1)} %bitcast.10, f32[1,256]{1,0:T(1,128)} %bitcast.12, f32[1,256]{1,0:T(1,128)} %bitcast.13), custom_call_target="tpu_custom_call" | custom-call | tf_op jit(solution)/shard_map/section/pallas_call | solution.py:426
  115.0 1.3 %fusion = (f32[1,256]{1,0:T(1,128)}, f32[1,256]{1,0:T(1,128)}) fusion(f32[8,256]{1,0:T(8,128)} %get-tuple-element.6), kind=kLoop, calls=%fused_computation | loop fusion | bytes 4096 | tf_op jit(solution)/shard_map/slice | solution.py:441
  116.4 6.7 %slice.12 = f32[27,256,256]{2,1,0:T(8,128)} slice(f32[28,256,256]{2,1,0:T(8,128)} %bitcast.9), slice={[0:27], [0:256], [0:256]} | slice | bytes 14155776 | tf_op jit(solution)/shard_map/slice | solution.py:440

commit v2 on v1

v2 whole, which is shorter than its diff:
```python
import functools

import jax
import jax.numpy as jnp
from jax import lax
from jax.experimental import pallas as pl
from jax.experimental.pallas import tpu as pltpu
from jax.sharding import PartitionSpec as P

MESH = pl.DeviceIdType.MESH
F32 = jnp.float32
BF16 = jnp.bfloat16
penalty_weight = 0.01
C = 256
NTM = 32
NREMOTE = 192


POWER = 16.0
SHIFT = 120.0
SPAN = 1200.0


def kernel(
    clips_hbm, w_hbm, bias_hbm, head_hbm, out_ref, small_ref,
    clips_ref, bias_ref, head_ref, wv, wt, slabs, xraw, xcat, sraw, shl, shr, scat, graw, ghl, ghr, gcat,
    scells, gcells, vals, acc, slope_s, curve_s, sg_s, pgb_s,
    xt, gt, xg, gg, ex, eg, rs_s, rs_p, total, gh, code,
    ry1, rz1, ry2, rz2, meta, mg, my, mz,
    local_sems, send_sems, recv_sems,
):
    dp = lax.axis_index("dp")
    tm = lax.axis_index("tm")
    x = lax.axis_index("rows")
    core = lax.rem(tm, 2)
    y = dp * 2 + lax.rem(tm // 2, 2)
    z = tm // 4
    has_prev = tm > 0
    has_next = tm < NTM - 1
    has_left = x > 0
    has_right = x < 3

    def dev(xx, yy, zz, cc):
        return (yy // 2, zz * 4 + lax.rem(yy, 2) * 2 + cc, xx)

    def xp(s):
        return lax.rem(x + s, 4)

    def yp(s):
        return lax.rem(y + s, 4)

    def zp(s):
        return lax.rem(z + s, 8)

    partner = dev(x, y, z, 1 - core)
    group = x * 2 + core
    chip = tm - core
    chip_prev = chip > 0
    chip_next = chip < NTM - 2

    def gp(s):
        return lax.rem(group + s, 8)

    def peer(s):
        return dev(gp(s) // 2, y, z, lax.rem(gp(s), 2))

    counter = [0]
    sends = []

    def remote(src, dst, target, recv=None):
        n = counter[0]
        counter[0] += 1
        assert n < NREMOTE
        return pltpu.make_async_remote_copy(
            src_ref=src, dst_ref=dst, send_sem=send_sems.at[n],
            recv_sem=recv_sems.at[n if recv is None else recv],
            device_id=target, device_id_type=MESH,
        )

    clips_in, bias_in, head_in, wcopy = arguments = [
        pltpu.make_async_copy(src, dst, local_sems.at[n])
        for n, (src, dst) in enumerate(
            ((clips_hbm, clips_ref), (bias_hbm, bias_ref), (head_hbm, head_ref), (w_hbm, wv))
        )
    ]
    for copy in arguments:
        copy.start()

    barrier = pltpu.get_barrier_semaphore()

    def greet(target):
        pl.semaphore_signal(barrier, inc=1, device_id=target, device_id_type=MESH)

    for s in range(1, 8):
        greet(peer(s))
        greet(dev(x, y, zp(s), core))
    for s in range(1, 4):
        greet(dev(x, yp(s), z, core))

    @pl.when(chip_prev)
    def _():
        for s in range(4):
            for q in range(2):
                greet((dp, chip - 2 + q, xp(s)))

    @pl.when(chip_next)
    def _():
        for s in range(4):
            for q in range(2):
                greet((dp, chip + 2 + q, xp(s)))

    zrow = jnp.zeros((4, 32, 768), BF16)
    for cat in (xcat, scat, gcat):
        cat[:, 0] = zrow
        cat[:, 5] = zrow

    @pl.when(jnp.logical_not(has_prev))
    def _():
        xraw[0] = jnp.zeros((4, 48, C), BF16)
        for raw, hl, hr in ((sraw, shl, shr), (graw, ghl, ghr)):
            raw[0] = jnp.zeros((4, 32, C), BF16)
            hl[0] = jnp.zeros((8, C), F32)
            hr[0] = jnp.zeros((8, C), F32)

    @pl.when(jnp.logical_not(has_next))
    def _():
        xraw[3] = jnp.zeros((4, 48, C), BF16)
        for raw, hl, hr in ((sraw, shl, shr), (graw, ghl, ghr)):
            raw[3] = jnp.zeros((4, 32, C), BF16)
            hl[3] = jnp.zeros((8, C), F32)
            hr[3] = jnp.zeros((8, C), F32)

    @pl.when(jnp.logical_not(has_left))
    def _():
        for hl in (shl, ghl):
            hl[...] = jnp.zeros((4, 8, C), F32)

    @pl.when(jnp.logical_not(has_right))
    def _():
        for hr in (shr, ghr):
            hr[...] = jnp.zeros((4, 8, C), F32)

    @pl.when(jnp.logical_not(chip_prev))
    def _():
        for field in (xg, gg):
            field[0] = jnp.zeros((4, 32, 128), BF16)

    @pl.when(jnp.logical_not(chip_next))
    def _():
        for field in (xg, gg):
            field[5] = jnp.zeros((4, 32, 128), BF16)

    for cells in (scells, gcells):
        cells[...] = jnp.zeros((2, 2, 8, C), F32)

    clips_in.wait()
    for f in range(2):
        v = clips_ref[f].astype(F32)
        edge = jnp.zeros((8, C), F32)
        v = jnp.concatenate([edge, v, edge], axis=0)
        for c in range(4):
            slabs[c, f] = v[32 * c:32 * c + 48].astype(BF16)
    xraw[1, x] = slabs[x, 0]
    xraw[2, x] = slabs[x, 1]
    pl.semaphore_wait(
        barrier, 17 + 8 * chip_prev.astype(jnp.int32) + 8 * chip_next.astype(jnp.int32)
    )

    same = [remote(slabs.at[xp(s)], xraw.at[pl.ds(1, 2), x], (dp, tm, xp(s))) for s in range(1, 4)]
    nxt = [remote(slabs.at[xp(s), 1], xraw.at[0, x], (dp, tm + 1, xp(s))) for s in range(4)]
    prv = [remote(slabs.at[xp(s), 0], xraw.at[3, x], (dp, tm - 1, xp(s))) for s in range(4)]

    def exchange(groups):
        for can_send, _, copies in groups:
            @pl.when(can_send)
            def _():
                for copy in copies:
                    copy.start()
        sends.extend((can_send, copies) for can_send, _, copies in groups)

    def arrive(groups):
        for _, can_receive, copies in groups:
            @pl.when(can_receive)
            def _():
                for copy in copies:
                    copy.wait_recv()

    always = tm >= 0
    first = ((always, always, same), (has_next, has_prev, nxt), (has_prev, has_next, prv))
    exchange(first)
    bias_in.wait()
    head_in.wait()
    wcopy.wait()
    for k in range(9):
        a, b = k // 3, k % 3
        for d in range(3):
            src = wv[(2 - a) * 3 + 2 - b, (2 - d) * 256:(3 - d) * 256]
            wt[k, d * 256:(d + 1) * 256] = src.T
    arrive(first)

    def first_cat(n, _):
        f, r = n // 4, lax.rem(n, 4)
        v = xraw[f, r].astype(F32)
        for d in range(3):
            xcat[f, r + 1, :, d * C:(d + 1) * C] = v[7 + d:39 + d].astype(BF16)
        return 0

    lax.fori_loop(0, 16, first_cat, 0)

    def conv(cat, weights):
        acc[...] = jnp.zeros((256, C), F32)

        def body(k, _):
            a, b = k // 3, lax.rem(k, 3)
            lhs = cat[pl.ds(a, 2), pl.ds(b, 4)].reshape(256, 768)
            acc[...] += jnp.dot(lhs, weights[k], preferred_element_type=F32)
            return 0

        lax.fori_loop(0, 9, body, 0)
        return acc[...]

    def halo(value, raw, hl, hr, cells):
        raw[1:3] = value.reshape(2, 4, 32, C)
        vals[...] = value.astype(F32).reshape(2, 4, 32, C)
        for f in range(2):
            for r in range(4):
                cells[0, f, r:r + 1] = vals[f, r, 0:1]
                cells[1, f, r:r + 1] = vals[f, r, 31:32]
        first_cells, last_cells = cells.at[0], cells.at[1]
        groups = (
            (has_next, has_prev, [remote(raw.at[2], raw.at[0], (dp, tm + 1, x))]),
            (has_prev, has_next, [remote(raw.at[1], raw.at[3], (dp, tm - 1, x))]),
            (has_right, has_left, [remote(last_cells, hl.at[pl.ds(1, 2)], (dp, tm, x + 1))]),
            (has_left, has_right, [remote(first_cells, hr.at[pl.ds(1, 2)], (dp, tm, x - 1))]),
            (has_next & has_right, has_prev & has_left, [remote(last_cells.at[1], hl.at[0], (dp, tm + 1, x + 1))]),
            (has_next & has_left, has_prev & has_right, [remote(first_cells.at[1], hr.at[0], (dp, tm + 1, x - 1))]),
            (has_prev & has_right, has_next & has_left, [remote(last_cells.at[0], hl.at[3], (dp, tm - 1, x + 1))]),
            (has_prev & has_left, has_next & has_right, [remote(first_cells.at[0], hr.at[3], (dp, tm - 1, x - 1))]),
        )
        exchange(groups)
        return groups

    def make_cat(raw, hl, hr, cat):
        def body(n, _):
            f, r = n // 4, lax.rem(n, 4)
            b = raw[f, r]
            v = b.astype(F32)
            row = lax.broadcasted_iota(jnp.int32, (32, C), 0)
            low = hl[f, pl.ds(r, 1)]
            high = hr[f, pl.ds(r, 1)]
            cat[f, r + 1, :, 0:C] = jnp.where(row == 0, low, pltpu.roll(v, 1, 0)).astype(BF16)
            cat[f, r + 1, :, C:2 * C] = b
            cat[f, r + 1, :, 2 * C:3 * C] = jnp.where(row == 31, high, pltpu.roll(v, 31, 0)).astype(BF16)
            return 0

        lax.fori_loop(0, 16, body, 0)

    def launch(copies):
        for copy in copies:
            copy.start()
        sends.append((always, copies))

    def landed(copies):
        for copy in copies:
            copy.wait_recv()

    def gather_left(center, turned, field):
        for f in range(2):
            turned[:, f] = center(f).T.reshape(8, 32, 128)
        for f in range(2):
            field[1 + 2 * core + f, x] = turned[group, f]
        near = [
            remote(turned.at[gp(s)], field.at[pl.ds(1 + 2 * core, 2), x], peer(s)) for s in range(1, 8)
        ]
        launch(near)
        up, down = [], []
        for s in range(4):
            for copies, frame, place, base in ((up, 1, 0, chip + 2), (down, 0, 5, chip - 2)):
                recv = None
                for q in range(2):
                    n = counter[0]
                    copies.append(remote(
                        turned.at[xp(s) * 2 + q, frame], field.at[place, x], (dp, base + q, xp(s)), recv
                    ))
                    recv = n if recv is None else recv
        edges = (
            (chip_next & (core == 1), chip_prev, up, up[::2]),
            (chip_prev & (core == 0), chip_next, down, down[::2]),
        )
        exchange(tuple(e[:3] for e in edges))
        return near, tuple((always, e[1], e[3]) for e in edges)

    def gather_right(value, field):
        own = pl.ds(2 * core, 2)
        for f in range(2):
            field[2 * core + f, x] = value[f]
        near = [remote(value, field.at[own, x], dev(xp(s), y, z, core)) for s in range(1, 4)]
        near.append(remote(value, field.at[own, x], partner))
        launch(near)
        hand = [remote(field.at[own, xp(4 - s)], field.at[own, xp(4 - s)], partner) for s in range(1, 4)]
        return near, hand

    def relay(near, hand):
        for copy, onward in zip(near[:3], hand):
            copy.wait_recv()
            onward.start()
        sends.append((always, hand))

    def gathered(near, hand):
        landed(near[3:])
        landed(hand)

    def expand(field, out):
        lane = lax.broadcasted_iota(jnp.int32, (32, 128), 1)
        col = lax.rem(lane, 32)

        def body(fi, _):
            v = [field[fi, c].astype(F32) for c in range(4)]
            none = jnp.zeros((32, 128), F32)
            for c in range(4):
                low = pltpu.roll(v[c - 1], 97, 1) if c > 0 else none
                high = pltpu.roll(v[c + 1], 31, 1) if c < 3 else none
                shifted = (
                    jnp.where(col == 0, low, pltpu.roll(v[c], 1, 1)),
                    v[c],
                    jnp.where(col == 31, high, pltpu.roll(v[c], 127, 1)),
                )
                for d in range(3):
                    w = shifted[d]
                    rows3 = (
                        jnp.where(lane < 32, 0.0, pltpu.roll(w, 32, 1)),
                        w,
                        jnp.where(lane >= 96, 0.0, pltpu.roll(w, 96, 1)),
                    )
                    for b in range(3):
                        out[b * 3 + d, fi, :, c * 128:(c + 1) * 128] = rows3[b].astype(BF16)
            return 0

        lax.fori_loop(0, 6, body, 0)

    def correlate(left, right):
        def body(t, _):
            lhs = left[:, pl.ds(t, 3)].reshape(864, 512)
            total[...] += jnp.dot(lhs, right[t].reshape(512, C), preferred_element_type=F32)
            return 0

        lax.fori_loop(0, 4, body, 0)

    pre = conv(xcat, wv) + bias_ref[...]
    sig = jax.nn.sigmoid(pre)
    slope = sig * (1.0 + pre * (1.0 - sig))
    slope_s[...] = slope
    curve_s[...] = sig * (1.0 - sig) * (2.0 + pre * (1.0 - 2.0 * sig))
    sg = (head_ref[...] * slope).astype(BF16)
    sg_s[...] = sg.reshape(2, 128, C)
    groups = halo(sg, sraw, shl, shr, scells)
    x_near, x_edges = gather_left(lambda f: xcat[1 + f, 1:5, :, C:2 * C].reshape(128, C), xt, xg)
    right_s = gather_right(sg_s, rs_s)
    arrive(groups)
    make_cat(sraw, shl, shr, scat)
    ig = conv(scat, wt).astype(BF16)
    groups = halo(ig, graw, ghl, ghr, gcells)
    relay(*right_s)
    g_near, g_edges = gather_left(lambda f: graw[1 + f].reshape(128, C), gt, gg)
    arrive(groups)
    make_cat(graw, ghl, ghr, gcat)
    back = penalty_weight * conv(gcat, wv)
    pre_grad = back * head_ref[...] * curve_s[...]
    pgb_s[...] = pre_grad.astype(BF16).reshape(2, 128, C)
    right_p = gather_right(pgb_s, rs_p)
    bias_row = jnp.sum(pre_grad, axis=0, keepdims=True)
    head_row = jnp.sum(back * slope_s[...], axis=0, keepdims=True)
    landed(g_near)
    arrive(g_edges)
    expand(gg, eg)
    gathered(*right_s)
    total[...] = jnp.zeros((864, C), F32)
    correlate(eg, rs_s)
    total[...] = penalty_weight * total[...]
    relay(*right_p)
    landed(x_near)
    arrive(x_edges)
    expand(xg, ex)
    gathered(*right_p)
    correlate(ex, rs_p)

    most = jnp.zeros((8, 128), F32)
    for tap in range(27):
        a, b, d = tap // 9, tap // 3 % 3, tap % 3
        n = (b * 3 + d) * 3 + a
        for h in range(2):
            block = total[n * 32:(n + 1) * 32, h * 128:(h + 1) * 128].reshape(4, 8, 128)
            gh[tap // 4, tap % 4, :, h] = block
            most = jnp.maximum(most, jnp.max(jnp.abs(block), axis=0))
    gh[6, 3] = jnp.zeros((4, 2, 8, 128), F32)
    tile = lax.broadcasted_iota(jnp.int32, (8, 128), 0)
    first_tile = jnp.zeros((8, 128), F32) + jnp.max(most)
    for n, row in enumerate((bias_row, head_row)):
        for h in range(2):
            first_tile = jnp.where(tile == 1 + 2 * n + h, row[:, h * 128:(h + 1) * 128], first_tile)

    zi, zh = z // 2, lax.rem(z, 2)
    Z = pl.ds(5, 2)
    y_spans = ((0, 2), (2, 3))
    one_y = [
        [remote(gh.at[pl.ds(*span), yp(s)], ry1.at[s - 1, pl.ds(*span)], dev(x, yp(s), z, core)) for s in range(1, 4)]
        for span in y_spans
    ]
    one_z = [
        remote(gh.at[Z, :, zp(s) // 2, lax.rem(zp(s), 2)], rz1.at[s - 1], dev(x, y, zp(s), core))
        for s in range(1, 8)
    ]
    launch(one_y[0])
    launch(one_z)
    launch(one_y[1])

    def spread(n, slots, me, targets):
        slots[me] = meta[n]
        copies = [remote(meta.at[n], slots.at[me], target) for target in targets]
        launch(copies)
        return copies

    def combine(n, slots, copies):
        landed(copies)
        new = slots[0]
        for s in range(1, slots.shape[0]):
            new = jnp.where(tile == 0, jnp.maximum(new, slots[s]), new + slots[s])
        meta[n + 1] = new

    meta[0] = first_tile
    meta_g = spread(0, mg, group, [peer(s) for s in range(1, 8)])
    combine(0, mg, meta_g)
    meta_y = spread(1, my, y, [dev(x, yp(s), z, core) for s in range(1, 4)])
    landed(one_z)
    t = gh[5:7, :, zi, zh]
    for s in range(7):
        t += rz1[s]
    gh[5:7, :, zi, zh] = t
    two_y = [remote(gh.at[Z, yp(s), zi, zh], ry2.at[s - 1], dev(x, yp(s), z, core)) for s in range(1, 4)]
    launch(two_y)
    combine(1, my, meta_y)
    meta_z = spread(2, mz, z, [dev(x, y, zp(s), core) for s in range(1, 8)])
    two_z = []
    for copies, (start, count) in zip(one_y, y_spans):
        landed(copies)
        for j in range(start, start + count):
            gh[j, y] += ry1[0, j] + ry1[1, j] + ry1[2, j]
        span = pl.ds(start, count)
        two_z.append([
            remote(gh.at[span, y, zp(s) // 2, lax.rem(zp(s), 2)], rz2.at[s - 1, span], dev(x, y, zp(s), core))
            for s in range(1, 8)
        ])
        launch(two_z[-1])
    combine(2, mz, meta_z)
    scale = SPAN / jnp.maximum(jnp.max(jnp.where(tile == 0, meta[3], 0.0)), 1e-30)

    def coded(v):
        u = v * scale
        w = jnp.exp2(POWER * jnp.log2(jnp.abs(u) + 1.0) - SHIFT)
        return jnp.where(u < 0.0, -w, w).astype(BF16)

    landed(two_y)
    t = gh[5:7, y, zi, zh] + ry2[0] + ry2[1] + ry2[2]
    code[5:7, y, x, core, zi, zh] = coded(t)
    piece = code.at[6, y, x, core, zi, zh]
    g1c = [remote(piece, piece, dev(x, yp(s), z, core)) for s in range(1, 4)]
    launch(g1c)
    landed(two_z[0])
    landed(two_z[1])
    t = gh[0:5, y, zi, zh]
    for s in range(7):
        t += rz2[s]
    code[0:5, y, x, core, zi, zh] = coded(t)

    A, B, AB = pl.ds(0, 3), pl.ds(3, 3), pl.ds(0, 6)
    piece = code.at[AB, y, x, core, zi, zh]
    g1z = [remote(piece, piece, dev(x, y, zp(s), core)) for s in range(1, 8)]
    launch(g1z)
    landed(g1c)
    piece = code.at[6, :, x, core, zi, zh]
    g2c = [remote(piece, piece, dev(xp(s), y, z, core)) for s in range(1, 4)]
    launch(g2c)
    landed(g1z)
    piece_a = code.at[A, y, x, core]
    g2a = [remote(piece_a, piece_a, dev(x, yp(s), z, core)) for s in range(1, 4)]
    launch(g2a)
    piece_b = code.at[B, y, x, core]
    g2b = [remote(piece_b, piece_b, dev(xp(s), y, z, core)) for s in range(1, 4)]
    launch(g2b)
    landed(g2c)
    piece_c = code.at[6, :, :, core, zi, zh]
    g3c = [remote(piece_c, piece_c, dev(x, y, zp(s), core)) for s in range(1, 8)]
    launch(g3c)
    landed(g2a)
    piece_a = code.at[A, :, x, core]
    g3a = [remote(piece_a, piece_a, dev(xp(s), y, z, core)) for s in range(1, 4)]
    launch(g3a)
    landed(g2b)
    piece_b = code.at[B, y, :, core]
    g3b = [remote(piece_b, piece_b, dev(x, yp(s), z, core)) for s in range(1, 4)]
    launch(g3b)
    small_ref[...] = jnp.zeros((8, C), F32)
    for h in range(2):
        lanes = slice(h * 128, (h + 1) * 128)
        small_ref[0:1, lanes] = meta[3, 1 + h:2 + h]
        small_ref[1:2, lanes] = meta[3, 3 + h:4 + h]
        small_ref[2:3, lanes] = jnp.zeros((1, 128), F32) + 1.0 / scale
    inverse = 1.0 / scale

    def decode(n, half):
        first, taps = ((0, 12), (12, 12), (24, 3))[n]

        def body(tap, _):
            for xx in range(4):
                for h in range(2):
                    w = code[tap // 4, lax.rem(tap, 4), xx, half, :, h].astype(F32).reshape(32, 128)
                    m = (jnp.exp2((jnp.log2(jnp.abs(w)) + SHIFT) * (1.0 / POWER)) - 1.0) * inverse
                    out_ref[tap, pl.ds(xx * 64 + half * 32, 32), h * 128:(h + 1) * 128] = jnp.where(w < 0.0, -m, m)
            return 0

        lax.fori_loop(first, first + taps, body, 0)

    spans = (A, B, pl.ds(6, 1))
    last = []
    for n, copies in ((2, g3c), (0, g3a), (1, g3b)):
        landed(copies)
        piece = code.at[spans[n], :, :, core]
        last.append((n, remote(piece, piece, partner)))
        launch([last[-1][1]])
    for n, _ in last:
        decode(n, core)
    for n, copy in last:
        copy.wait_recv()
        decode(n, 1 - core)
    for can_send, copies in sends:
        @pl.when(can_send)
        def _():
            for copy in copies:
                copy.wait_send()


PARTS = 9


def put(gw_ref, small_ref, out_hbm, bias_ref, head_ref, sems):
    size = 27 // PARTS
    copies = [
        pltpu.make_async_copy(gw_ref.at[pl.ds(n * size, size)], out_hbm.at[pl.ds(n * size, size)], sems.at[n])
        for n in range(PARTS)
    ]
    for copy in copies:
        copy.start()
    bias_ref[...] = small_ref[0:1]
    head_ref[...] = small_ref[1:2]
    for copy in copies:
        copy.wait()


def per_device(clips, weight, bias, head):
    vm = pltpu.VMEM
    field = lambda w: vm((4, 4, w, C), BF16)
    cells = vm((4, 8, C), F32)
    cat = vm((4, 6, 32, 768), BF16)
    plane = vm((256, C), F32)
    turned, left = vm((8, 2, 32, 128), BF16), vm((6, 4, 32, 128), BF16)
    wide, right = vm((9, 6, 32, 512), BF16), vm((4, 4, 128, C), BF16)
    coded = (7, 4, 4, 2, 4, 2, 8, 128)
    scratch = [
        vm((2, 128, C), BF16), vm((1, C), F32), vm((1, C), F32),
        vm((9, 768, C), BF16), vm((9, 768, C), BF16), vm((4, 2, 48, C), BF16), field(48), cat,
        field(32), cells, cells, cat, field(32), cells, cells, cat,
        vm((2, 2, 8, C), F32), vm((2, 2, 8, C), F32), vm((2, 4, 32, C), F32), plane, plane, plane,
        vm((2, 128, C), BF16), vm((2, 128, C), BF16),
        turned, turned, left, left, wide, wide, right, right, vm((864, C), F32),
        vm((7, 4, 4, 2, 8, 128), F32), vm(coded, BF16),
        vm((3, 5, 4, 2, 8, 128), F32), vm((7, 2, 4, 8, 128), F32), vm((3, 2, 8, 128), F32),
        vm((7, 5, 8, 128), F32),
        vm((4, 8, 128), F32), vm((8, 8, 128), F32), vm((4, 8, 128), F32), vm((8, 8, 128), F32),
        pltpu.SemaphoreType.DMA((4,)),
        pltpu.SemaphoreType.DMA((NREMOTE,)), pltpu.SemaphoreType.DMA((NREMOTE,)),
    ]
    inside = pl.BlockSpec(memory_space=pltpu.VMEM)
    outside = pl.BlockSpec(memory_space=pltpu.HBM)
    gw, small = pl.pallas_call(
        kernel,
        out_shape=(pltpu.VMEM((27, C, C), F32), pltpu.VMEM((8, C), F32)),
        in_specs=[outside] * 4,
        out_specs=(inside, inside),
        scratch_shapes=scratch,
        compiler_params=pltpu.CompilerParams(
            collective_id=0, has_side_effects=True, vmem_limit_bytes=48 * 1024 * 1024
        ),
        name="section",
    )(clips.reshape(2, 128, C), weight.reshape(9, 768, C), bias.reshape(1, C), head.reshape(1, C))
    gw, grad_bias, grad_head = pl.pallas_call(
        put,
        out_shape=(
            jax.ShapeDtypeStruct((27, C, C), F32),
            jax.ShapeDtypeStruct((1, C), F32),
            jax.ShapeDtypeStruct((1, C), F32),
        ),
        in_specs=[inside, inside],
        out_specs=(outside, inside, inside),
        scratch_shapes=[pltpu.SemaphoreType.DMA((PARTS,))],
        compiler_params=pltpu.CompilerParams(vmem_limit_bytes=16 * 1024 * 1024),
        name="put",
    )(gw, small)
    return gw.reshape(3, 3, 3, C, C), grad_bias.reshape(C), grad_head.reshape(C)


def solution(mesh):
    return jax.shard_map(
        per_device,
        mesh=mesh,
        in_specs=(P("dp", "tm", "rows", None, None), P(), P(), P()),
        out_specs=(P(), P(), P()),
        check_vma=False,
    )
```

time: 123 us -> 93.6 us (0.76)
  Pallas kernels: 114 us -> 92.8 us
  local copies, waits for them, and re-layouts: 8.07 us -> 0 us
    pallas_call x1 -> x2, Pallas kernels: 114 us -> 92.8 us  [the longest x1 89.3 us: per_device(): pl.pallas_call(kernel, out_shape=(pltpu.VMEM((27, C, C), F32), pltpu.VMEM...]
    slice x2 -> x0, local copies, waits for them, and re-layouts: 8.07 us -> none  [the longest x1 6.73 us: per_device(): grad_weight = gw.reshape(28, C, C)[:27].reshape(3, 3, 3, C, C)]
where the time goes in v2:
time: 93.6 us; the launch traced here: 93.5 us
  Pallas kernels  92.8 us (99%)
    pallas_call x1, Pallas kernels, per_device(): pl.pallas_call(kernel, out_shape=(pltpu.VMEM((27, C, C), F32), pltpu.VMEM...  89.3 us
    pallas_call x1, Pallas kernels, per_device(): pl.pallas_call(put, out_shape=(jax.ShapeDtypeStruct((27, C, C), F32), jax...  3.55 us

profile of v2, /device:TPU:1, one launch (start us, length us, event | category | flops | bytes accessed | tf_op | source)
XLA Modules:
  0.0 93.5 jit_solution(14020899767836271373)
XLA Ops:
  0.6 89.3 %section.1 = (f32[27,256,256]{2,1,0:T(8,128)S(1)}, f32[8,256]{1,0:T(8,128)S(1)}) custom-call(bf16[2,128,256]{2,1,0:T(8,128)(2,1)} %bitcast.8, bf16[9,768,256]{2,1,0:T(8,128)(2,1)} %bitcast.7, f32[1,256]{1,0:T(1,128)} %bitcast.9, f32[1,256]{1,0:T(1,128)} %bitcast.10), custom_call_target="tpu_custom_call" | custom-call | tf_op jit(solution)/shard_map/section/pallas_call | solution.py:584
  89.9 3.6 %put.1 = (f32[27,256,256]{2,1,0:T(8,128)}, f32[1,256]{1,0:T(1,128)}, f32[1,256]{1,0:T(1,128)}) custom-call(f32[27,256,256]{2,1,0:T(8,128)S(1)} %get-tuple-element.8.gw_ref, f32[8,256]{1,0:T(8,128)S(1)} %get-tuple-element.9.small_ref), custom_call_target="tpu_custom_call" | custom-call | tf_op jit(solution)/shard_map/put/pallas_call | solution.py:595

commit v3 on v2

--- a/solution.py
+++ b/solution.py
@@ -13,7 +13,7 @@
 penalty_weight = 0.01
 C = 256
 NTM = 32
-NREMOTE = 192
+NREMOTE = 224
 
 
 POWER = 16.0
@@ -360,7 +360,6 @@
     make_cat(sraw, shl, shr, scat)
     ig = conv(scat, wt).astype(BF16)
     groups = halo(ig, graw, ghl, ghr, gcells)
-    relay(*right_s)
     g_near, g_edges = gather_left(lambda f: graw[1 + f].reshape(128, C), gt, gg)
     arrive(groups)
     make_cat(graw, ghl, ghr, gcat)
@@ -368,6 +367,7 @@
     pre_grad = back * head_ref[...] * curve_s[...]
     pgb_s[...] = pre_grad.astype(BF16).reshape(2, 128, C)
     right_p = gather_right(pgb_s, rs_p)
+    relay(*right_s)
     bias_row = jnp.sum(pre_grad, axis=0, keepdims=True)
     head_row = jnp.sum(back * slope_s[...], axis=0, keepdims=True)
     landed(g_near)
@@ -400,19 +400,19 @@
             first_tile = jnp.where(tile == 1 + 2 * n + h, row[:, h * 128:(h + 1) * 128], first_tile)
 
     zi, zh = z // 2, lax.rem(z, 2)
-    Z = pl.ds(5, 2)
-    y_spans = ((0, 2), (2, 3))
+    Z = pl.ds(0, 2)
+    y_spans = ((4, 3), (2, 2))
     one_y = [
-        [remote(gh.at[pl.ds(*span), yp(s)], ry1.at[s - 1, pl.ds(*span)], dev(x, yp(s), z, core)) for s in range(1, 4)]
-        for span in y_spans
+        [
+            remote(gh.at[pl.ds(j, n), yp(s)], ry1.at[s - 1, pl.ds(j - 2, n)], dev(x, yp(s), z, core))
+            for s in range(1, 4)
+        ]
+        for j, n in y_spans
     ]
     one_z = [
         remote(gh.at[Z, :, zp(s) // 2, lax.rem(zp(s), 2)], rz1.at[s - 1], dev(x, y, zp(s), core))
         for s in range(1, 8)
     ]
-    launch(one_y[0])
-    launch(one_z)
-    launch(one_y[1])
 
     def spread(n, slots, me, targets):
         slots[me] = meta[n]
@@ -428,110 +428,170 @@
         meta[n + 1] = new
 
     meta[0] = first_tile
-    meta_g = spread(0, mg, group, [peer(s) for s in range(1, 8)])
-    combine(0, mg, meta_g)
-    meta_y = spread(1, my, y, [dev(x, yp(s), z, core) for s in range(1, 4)])
-    landed(one_z)
-    t = gh[5:7, :, zi, zh]
-    for s in range(7):
-        t += rz1[s]
-    gh[5:7, :, zi, zh] = t
-    two_y = [remote(gh.at[Z, yp(s), zi, zh], ry2.at[s - 1], dev(x, yp(s), z, core)) for s in range(1, 4)]
-    launch(two_y)
-    combine(1, my, meta_y)
-    meta_z = spread(2, mz, z, [dev(x, y, zp(s), core) for s in range(1, 8)])
+    meta_y = spread(0, my, y, [dev(x, yp(s), z, core) for s in range(1, 4)])
+    launch(one_y[0])
+    launch(one_z)
+    launch(one_y[1])
+    combine(0, my, meta_y)
+    meta_z = spread(1, mz, z, [dev(x, y, zp(s), core) for s in range(1, 8)])
     two_z = []
     for copies, (start, count) in zip(one_y, y_spans):
         landed(copies)
         for j in range(start, start + count):
-            gh[j, y] += ry1[0, j] + ry1[1, j] + ry1[2, j]
-        span = pl.ds(start, count)
+            gh[j, y] += ry1[0, j - 2] + ry1[1, j - 2] + ry1[2, j - 2]
         two_z.append([
-            remote(gh.at[span, y, zp(s) // 2, lax.rem(zp(s), 2)], rz2.at[s - 1, span], dev(x, y, zp(s), core))
+            remote(
+                gh.at[pl.ds(start, count), y, zp(s) // 2, lax.rem(zp(s), 2)],
+                rz2.at[s - 1, pl.ds(start - 2, count)], dev(x, y, zp(s), core),
+            )
             for s in range(1, 8)
         ])
         launch(two_z[-1])
-    combine(2, mz, meta_z)
-    scale = SPAN / jnp.maximum(jnp.max(jnp.where(tile == 0, meta[3], 0.0)), 1e-30)
+    landed(one_z)
+    t = gh[0:2, :, zi, zh]
+    for s in range(7):
+        t += rz1[s]
+    gh[0:2, :, zi, zh] = t
+    two_y = [remote(gh.at[Z, yp(s), zi, zh], ry2.at[s - 1], dev(x, yp(s), z, core)) for s in range(1, 4)]
+    launch(two_y)
+    combine(1, mz, meta_z)
+    meta_g = spread(2, mg, group, [peer(s) for s in range(1, 8)])
+    scale = SPAN / jnp.clip(jnp.max(jnp.where(tile == 0, meta[2], 0.0)), 1e-30, 1e30)
+    scale = (jnp.zeros((8, 128), F32) + scale).astype(BF16).astype(F32)
 
     def coded(v):
         u = v * scale
         w = jnp.exp2(POWER * jnp.log2(jnp.abs(u) + 1.0) - SHIFT)
         return jnp.where(u < 0.0, -w, w).astype(BF16)
 
+    def close(n):
+        start, count = y_spans[n]
+        landed(two_z[n])
+        t = gh[start:start + count, y, zi, zh]
+        for s in range(7):
+            t += rz2[s, start - 2:start - 2 + count]
+        return coded(t)
+
+    def pair_z(j):
+        piece = code.at[pl.ds(j, 2), y, x, core, zi, zh]
+        copies = [remote(piece, piece, dev(x, y, zp(s), core)) for s in range(1, 8)]
+        launch(copies)
+        return copies
+
+    def pair_two(j):
+        a, b = code.at[j, y, x, core], code.at[j + 1, y, x, core]
+        copies = [remote(a, a, dev(x, yp(s), z, core)) for s in range(1, 4)]
+        copies += [remote(b, b, dev(xp(s), y, z, core)) for s in range(1, 4)]
+        launch(copies)
+        return copies
+
+    def pair_three(j):
+        a, b = code.at[j, :, x, core], code.at[j + 1, y, :, core]
+        one = [remote(a, a, dev(xp(s), y, z, core)) for s in range(1, 4)]
+        two = [remote(b, b, dev(x, yp(s), z, core)) for s in range(1, 4)]
+        launch(one + two)
+        return one, two
+
+    t = close(0)
+    code[4:6, y, x, core, zi, zh] = t[0:2]
+    code[6, y, x, core, zi, zh] = jnp.where(y == 3, scale, t[2].astype(F32)).astype(BF16)
+    early = pair_z(5)
+    piece = code.at[4, y, x, core, zi, zh]
+    c1 = [remote(piece, piece, dev(x, yp(s), z, core)) for s in range(1, 4)]
+    launch(c1)
     landed(two_y)
-    t = gh[5:7, y, zi, zh] + ry2[0] + ry2[1] + ry2[2]
-    code[5:7, y, x, core, zi, zh] = coded(t)
-    piece = code.at[6, y, x, core, zi, zh]
-    g1c = [remote(piece, piece, dev(x, yp(s), z, core)) for s in range(1, 4)]
-    launch(g1c)
-    landed(two_z[0])
-    landed(two_z[1])
-    t = gh[0:5, y, zi, zh]
-    for s in range(7):
-        t += rz2[s]
-    code[0:5, y, x, core, zi, zh] = coded(t)
-
-    A, B, AB = pl.ds(0, 3), pl.ds(3, 3), pl.ds(0, 6)
-    piece = code.at[AB, y, x, core, zi, zh]
-    g1z = [remote(piece, piece, dev(x, y, zp(s), core)) for s in range(1, 8)]
-    launch(g1z)
-    landed(g1c)
-    piece = code.at[6, :, x, core, zi, zh]
-    g2c = [remote(piece, piece, dev(xp(s), y, z, core)) for s in range(1, 4)]
-    launch(g2c)
-    landed(g1z)
-    piece_a = code.at[A, y, x, core]
-    g2a = [remote(piece_a, piece_a, dev(x, yp(s), z, core)) for s in range(1, 4)]
-    launch(g2a)
-    piece_b = code.at[B, y, x, core]
-    g2b = [remote(piece_b, piece_b, dev(xp(s), y, z, core)) for s in range(1, 4)]
-    launch(g2b)
-    landed(g2c)
-    piece_c = code.at[6, :, :, core, zi, zh]
-    g3c = [remote(piece_c, piece_c, dev(x, y, zp(s), core)) for s in range(1, 8)]
-    launch(g3c)
-    landed(g2a)
-    piece_a = code.at[A, :, x, core]
-    g3a = [remote(piece_a, piece_a, dev(xp(s), y, z, core)) for s in range(1, 4)]
-    launch(g3a)
-    landed(g2b)
-    piece_b = code.at[B, y, :, core]
-    g3b = [remote(piece_b, piece_b, dev(x, yp(s), z, core)) for s in range(1, 4)]
-    launch(g3b)
+    code[0:2, y, x, core, zi, zh] = coded(gh[0:2, y, zi, zh] + ry2[0] + ry2[1] + ry2[2])
+    other = pair_z(0)
+    landed(c1)
+    piece = code.at[4, :, x, core, zi, zh]
+    c2 = [remote(piece, piece, dev(xp(s), y, z, core)) for s in range(1, 4)]
+    launch(c2)
+    code[2:4, y, x, core, zi, zh] = close(1)
+    late = pair_z(2)
+    landed(early)
+    early = pair_two(5)
+    landed(c2)
+    piece = code.at[4, :, :, core, zi, zh]
+    c3 = [remote(piece, piece, dev(x, y, zp(s), core)) for s in range(1, 8)]
+    launch(c3)
+    landed(other)
+    other = pair_two(0)
+    landed(early)
+    early = pair_three(5)
+    landed(late)
+    late = pair_two(2)
+    landed(other)
+    other = pair_three(0)
+    landed(late)
+    late_a, late_b = pair_three(2)
+    combine(2, mg, meta_g)
     small_ref[...] = jnp.zeros((8, C), F32)
     for h in range(2):
         lanes = slice(h * 128, (h + 1) * 128)
         small_ref[0:1, lanes] = meta[3, 1 + h:2 + h]
         small_ref[1:2, lanes] = meta[3, 3 + h:4 + h]
-        small_ref[2:3, lanes] = jnp.zeros((1, 128), F32) + 1.0 / scale
-    inverse = 1.0 / scale
-
-    def decode(n, half):
-        first, taps = ((0, 12), (12, 12), (24, 3))[n]
-
-        def body(tap, _):
-            for xx in range(4):
-                for h in range(2):
-                    w = code[tap // 4, lax.rem(tap, 4), xx, half, :, h].astype(F32).reshape(32, 128)
-                    m = (jnp.exp2((jnp.log2(jnp.abs(w)) + SHIFT) * (1.0 / POWER)) - 1.0) * inverse
-                    out_ref[tap, pl.ds(xx * 64 + half * 32, 32), h * 128:(h + 1) * 128] = jnp.where(w < 0.0, -m, m)
+
+    def decode(first, js, t0, ts, x0, xs, half):
+        def body(n, _):
+            j, t, xx = first + n // (ts * xs), t0 + lax.rem(n // xs, ts), x0 + lax.rem(n, xs)
+            inverse = 1.0 / code[6, 3, xx, half, 0, 0].astype(F32)[0:1]
+            for h in range(2):
+                w = code[j, t, xx, half, :, h].astype(F32).reshape(32, 128)
+                m = (jnp.exp2((jnp.log2(jnp.abs(w)) + SHIFT) * (1.0 / POWER)) - 1.0) * inverse
+                out_ref[j * 4 + t, pl.ds(xx * 64 + half * 32, 32), h * 128:(h + 1) * 128] = jnp.where(w < 0.0, -m, m)
             return 0
 
-        lax.fori_loop(first, first + taps, body, 0)
-
-    spans = (A, B, pl.ds(6, 1))
-    last = []
-    for n, copies in ((2, g3c), (0, g3a), (1, g3b)):
-        landed(copies)
-        piece = code.at[spans[n], :, :, core]
-        last.append((n, remote(piece, piece, partner)))
-        launch([last[-1][1]])
-    for n, _ in last:
-        decode(n, core)
-    for n, copy in last:
+        lax.fori_loop(0, js * ts * xs, body, 0)
+
+    handed = []
+
+    def hand(j, js, t, ts, xx, xs):
+        piece = code.at[pl.ds(j, js), pl.ds(t, ts), pl.ds(xx, xs), core]
+        copy = remote(piece, piece, partner)
+        launch([copy])
+        handed.append((copy, j, js, t, ts, xx, xs))
+
+    def show(j, js, t, ts, xx, xs, half):
+        if j + js == 7:
+            decode(5, 1, t, ts, xx, xs, half)
+            decode(6, 1, 0, 3, xx, xs, half)
+        else:
+            decode(j, js, t, ts, xx, xs, half)
+
+    def finish():
+        copy, *place = handed.pop(0)
         copy.wait_recv()
-        decode(n, 1 - core)
+        show(*place, 1 - core)
+
+    hand(2, 1, 0, 4, x, 1)
+    hand(3, 1, y, 1, 0, 4)
+    landed(early[0] + early[1])
+    handed, waiting = [], handed
+    hand(5, 2, 0, 4, 0, 4)
+    show(5, 2, 0, 4, 0, 4, core)
+    landed(c3)
+    hand(4, 1, 0, 4, 0, 4)
+    show(4, 1, 0, 4, 0, 4, core)
+    landed(other[0] + other[1])
+    hand(0, 2, 0, 4, 0, 4)
+    finish()
+    handed += waiting
+    show(2, 1, 0, 4, x, 1, core)
+    show(3, 1, y, 1, 0, 4, core)
+    for s in (1, 3, 2):
+        late_a[s - 1].wait_recv()
+        hand(2, 1, 0, 4, xp(4 - s), 1)
+        late_b[s - 1].wait_recv()
+        hand(3, 1, yp(4 - s), 1, 0, 4)
+        if s == 1:
+            show(0, 2, 0, 4, 0, 4, core)
+            finish()
+        show(2, 1, 0, 4, xp(4 - s), 1, core)
+        show(3, 1, yp(4 - s), 1, 0, 4, core)
+        if s == 3:
+            finish()
+    while handed:
+        finish()
     for can_send, copies in sends:
         @pl.when(can_send)
         def _():

time: 93.6 us -> 91.9 us (0.982)
  Pallas kernels: 92.8 us -> 91.2 us
    pallas_call x1, Pallas kernels: 89.3 us -> 87.6 us  [per_device(): pl.pallas_call(kernel, out_shape=(pltpu.VMEM((27, C, C), F32), pltpu.VMEM...]
where the time goes in v3:
time: 91.9 us; the launch traced here: 91.8 us
  Pallas kernels  91.2 us (99%)
    pallas_call x1, Pallas kernels, per_device(): pl.pallas_call(kernel, out_shape=(pltpu.VMEM((27, C, C), F32), pltpu.VMEM...  87.6 us
    pallas_call x1, Pallas kernels, per_device(): pl.pallas_call(put, out_shape=(jax.ShapeDtypeStruct((27, C, C), F32), jax...  3.55 us

profile of v3, /device:TPU:1, one launch (start us, length us, event | category | flops | bytes accessed | tf_op | source)
XLA Modules:
  0.0 91.8 jit_solution(2757768712070484834)
XLA Ops:
  0.6 87.6 %section.1 = (f32[27,256,256]{2,1,0:T(8,128)S(1)}, f32[8,256]{1,0:T(8,128)S(1)}) custom-call(bf16[2,128,256]{2,1,0:T(8,128)(2,1)} %bitcast.8, bf16[9,768,256]{2,1,0:T(8,128)(2,1)} %bitcast.7, f32[1,256]{1,0:T(1,128)} %bitcast.9, f32[1,256]{1,0:T(1,128)} %bitcast.10), custom_call_target="tpu_custom_call" | custom-call | tf_op jit(solution)/shard_map/section/pallas_call | solution.py:644
  88.2 3.6 %put.1 = (f32[27,256,256]{2,1,0:T(8,128)}, f32[1,256]{1,0:T(1,128)}, f32[1,256]{1,0:T(1,128)}) custom-call(f32[27,256,256]{2,1,0:T(8,128)S(1)} %get-tuple-element.8.gw_ref, f32[8,256]{1,0:T(8,128)S(1)} %get-tuple-element.9.small_ref), custom_call_target="tpu_custom_call" | custom-call | tf_op jit(solution)/shard_map/put/pallas_call | solution.py:655

commit v4 on v3

--- a/solution.py
+++ b/solution.py
@@ -18,11 +18,12 @@
 
 POWER = 16.0
 SHIFT = 120.0
+ROOT = 2.0 ** (SHIFT / POWER)
 SPAN = 1200.0
 
 
 def kernel(
-    clips_hbm, w_hbm, bias_hbm, head_hbm, out_ref, small_ref,
+    clips_hbm, w_hbm, bias_hbm, head_hbm, out_ref, bias_out, head_out,
     clips_ref, bias_ref, head_ref, wv, wt, slabs, xraw, xcat, sraw, shl, shr, scat, graw, ghl, ghr, gcat,
     scells, gcells, vals, acc, slope_s, curve_s, sg_s, pgb_s,
     xt, gt, xg, gg, ex, eg, rs_s, rs_p, total, gh, code,
@@ -116,7 +117,7 @@
 
     @pl.when(jnp.logical_not(has_prev))
     def _():
-        xraw[0] = jnp.zeros((4, 48, C), BF16)
+        xraw[0] = jnp.zeros((4, 40, C), BF16)
         for raw, hl, hr in ((sraw, shl, shr), (graw, ghl, ghr)):
             raw[0] = jnp.zeros((4, 32, C), BF16)
             hl[0] = jnp.zeros((8, C), F32)
@@ -124,7 +125,7 @@
 
     @pl.when(jnp.logical_not(has_next))
     def _():
-        xraw[3] = jnp.zeros((4, 48, C), BF16)
+        xraw[3] = jnp.zeros((4, 40, C), BF16)
         for raw, hl, hr in ((sraw, shl, shr), (graw, ghl, ghr)):
             raw[3] = jnp.zeros((4, 32, C), BF16)
             hl[3] = jnp.zeros((8, C), F32)
@@ -159,7 +160,7 @@
         edge = jnp.zeros((8, C), F32)
         v = jnp.concatenate([edge, v, edge], axis=0)
         for c in range(4):
-            slabs[c, f] = v[32 * c:32 * c + 48].astype(BF16)
+            slabs[c, f] = v[32 * c + 7:32 * c + 47].astype(BF16)
     xraw[1, x] = slabs[x, 0]
     xraw[2, x] = slabs[x, 1]
     pl.semaphore_wait(
@@ -202,22 +203,19 @@
         f, r = n // 4, lax.rem(n, 4)
         v = xraw[f, r].astype(F32)
         for d in range(3):
-            xcat[f, r + 1, :, d * C:(d + 1) * C] = v[7 + d:39 + d].astype(BF16)
+            xcat[f, r + 1, :, d * C:(d + 1) * C] = v[d:32 + d].astype(BF16)
         return 0
 
-    lax.fori_loop(0, 16, first_cat, 0)
+    lax.fori_loop(0, 16, first_cat, 0, unroll=4)
 
     def conv(cat, weights):
-        acc[...] = jnp.zeros((256, C), F32)
-
-        def body(k, _):
-            a, b = k // 3, lax.rem(k, 3)
-            lhs = cat[pl.ds(a, 2), pl.ds(b, 4)].reshape(256, 768)
-            acc[...] += jnp.dot(lhs, weights[k], preferred_element_type=F32)
-            return 0
-
-        lax.fori_loop(0, 9, body, 0)
-        return acc[...]
+        value = None
+        for k in range(9):
+            a, b = k // 3, k % 3
+            lhs = cat[a:a + 2, b:b + 4].reshape(256, 768)
+            part = jnp.dot(lhs, weights[k], preferred_element_type=F32)
+            value = part if value is None else value + part
+        return value
 
     def halo(value, raw, hl, hr, cells):
         raw[1:3] = value.reshape(2, 4, 32, C)
@@ -253,7 +251,7 @@
             cat[f, r + 1, :, 2 * C:3 * C] = jnp.where(row == 31, high, pltpu.roll(v, 31, 0)).astype(BF16)
             return 0
 
-        lax.fori_loop(0, 16, body, 0)
+        lax.fori_loop(0, 16, body, 0, unroll=4)
 
     def launch(copies):
         for copy in copies:
@@ -525,23 +523,23 @@
     landed(late)
     late_a, late_b = pair_three(2)
     combine(2, mg, meta_g)
-    small_ref[...] = jnp.zeros((8, C), F32)
     for h in range(2):
         lanes = slice(h * 128, (h + 1) * 128)
-        small_ref[0:1, lanes] = meta[3, 1 + h:2 + h]
-        small_ref[1:2, lanes] = meta[3, 3 + h:4 + h]
+        bias_out[:, lanes] = meta[3, 1 + h:2 + h]
+        head_out[:, lanes] = meta[3, 3 + h:4 + h]
 
     def decode(first, js, t0, ts, x0, xs, half):
         def body(n, _):
             j, t, xx = first + n // (ts * xs), t0 + lax.rem(n // xs, ts), x0 + lax.rem(n, xs)
             inverse = 1.0 / code[6, 3, xx, half, 0, 0].astype(F32)[0:1]
+            grown = inverse * ROOT
             for h in range(2):
                 w = code[j, t, xx, half, :, h].astype(F32).reshape(32, 128)
-                m = (jnp.exp2((jnp.log2(jnp.abs(w)) + SHIFT) * (1.0 / POWER)) - 1.0) * inverse
+                m = lax.rsqrt(lax.rsqrt(lax.rsqrt(lax.rsqrt(jnp.abs(w))))) * grown - inverse
                 out_ref[j * 4 + t, pl.ds(xx * 64 + half * 32, 32), h * 128:(h + 1) * 128] = jnp.where(w < 0.0, -m, m)
             return 0
 
-        lax.fori_loop(0, js * ts * xs, body, 0)
+        lax.fori_loop(0, js * ts * xs, body, 0, unroll=4 if js * ts * xs % 4 == 0 else 1)
 
     handed = []
 
@@ -602,16 +600,16 @@
 PARTS = 9
 
 
-def put(gw_ref, small_ref, out_hbm, bias_ref, head_ref, sems):
+def put(gw_ref, bias_ref, head_ref, out_hbm, bias_hbm, head_hbm, sems):
     size = 27 // PARTS
     copies = [
         pltpu.make_async_copy(gw_ref.at[pl.ds(n * size, size)], out_hbm.at[pl.ds(n * size, size)], sems.at[n])
         for n in range(PARTS)
     ]
+    copies.append(pltpu.make_async_copy(bias_ref, bias_hbm, sems.at[PARTS]))
+    copies.append(pltpu.make_async_copy(head_ref, head_hbm, sems.at[PARTS + 1]))
     for copy in copies:
         copy.start()
-    bias_ref[...] = small_ref[0:1]
-    head_ref[...] = small_ref[1:2]
     for copy in copies:
         copy.wait()
 
@@ -627,7 +625,7 @@
     coded = (7, 4, 4, 2, 4, 2, 8, 128)
     scratch = [
         vm((2, 128, C), BF16), vm((1, C), F32), vm((1, C), F32),
-        vm((9, 768, C), BF16), vm((9, 768, C), BF16), vm((4, 2, 48, C), BF16), field(48), cat,
+        vm((9, 768, C), BF16), vm((9, 768, C), BF16), vm((4, 2, 40, C), BF16), field(40), cat,
         field(32), cells, cells, cat, field(32), cells, cells, cat,
         vm((2, 2, 8, C), F32), vm((2, 2, 8, C), F32), vm((2, 4, 32, C), F32), plane, plane, plane,
         vm((2, 128, C), BF16), vm((2, 128, C), BF16),
@@ -641,11 +639,11 @@
     ]
     inside = pl.BlockSpec(memory_space=pltpu.VMEM)
     outside = pl.BlockSpec(memory_space=pltpu.HBM)
-    gw, small = pl.pallas_call(
+    gw, grad_bias, grad_head = pl.pallas_call(
         kernel,
-        out_shape=(pltpu.VMEM((27, C, C), F32), pltpu.VMEM((8, C), F32)),
+        out_shape=(pltpu.VMEM((27, C, C), F32), pltpu.VMEM((1, C), F32), pltpu.VMEM((1, C), F32)),
         in_specs=[outside] * 4,
-        out_specs=(inside, inside),
+        out_specs=(inside, inside, inside),
         scratch_shapes=scratch,
         compiler_params=pltpu.CompilerParams(
             collective_id=0, has_side_effects=True, vmem_limit_bytes=48 * 1024 * 1024
@@ -659,12 +657,12 @@
             jax.ShapeDtypeStruct((1, C), F32),
             jax.ShapeDtypeStruct((1, C), F32),
         ),
-        in_specs=[inside, inside],
-        out_specs=(outside, inside, inside),
-        scratch_shapes=[pltpu.SemaphoreType.DMA((PARTS,))],
+        in_specs=[inside, inside, inside],
+        out_specs=(outside, outside, outside),
+        scratch_shapes=[pltpu.SemaphoreType.DMA((PARTS + 2,))],
         compiler_params=pltpu.CompilerParams(vmem_limit_bytes=16 * 1024 * 1024),
         name="put",
-    )(gw, small)
+    )(gw, grad_bias, grad_head)
     return gw.reshape(3, 3, 3, C, C), grad_bias.reshape(C), grad_head.reshape(C)
 
 

time: 91.9 us -> 87.6 us (0.953)
  Pallas kernels: 91.2 us -> 86.9 us
    pallas_call x1, Pallas kernels: 87.6 us -> 83.9 us  [per_device(): pl.pallas_call(kernel, out_shape=(pltpu.VMEM((27, C, C), F32), pltpu.VMEM...]
where the time goes in v4:
time: 87.6 us; the launch traced here: 87.5 us
  Pallas kernels  86.9 us (99%)
    pallas_call x1, Pallas kernels, per_device(): pl.pallas_call(kernel, out_shape=(pltpu.VMEM((27, C, C), F32), pltpu.VMEM...  83.9 us
    pallas_call x1, Pallas kernels, per_device(): pl.pallas_call(put, out_shape=(jax.ShapeDtypeStruct((27, C, C), F32), jax...  3.01 us

profile of v4, /device:TPU:1, one launch (start us, length us, event | category | flops | bytes accessed | tf_op | source)
XLA Modules:
  0.0 87.5 jit_solution(1524890904120935279)
XLA Ops:
  0.6 83.9 %section.1 = (f32[27,256,256]{2,1,0:T(8,128)S(1)}, f32[1,256]{1,0:T(1,128)S(1)}, f32[1,256]{1,0:T(1,128)S(1)}) custom-call(bf16[2,128,256]{2,1,0:T(8,128)(2,1)} %bitcast.8, bf16[9,768,256]{2,1,0:T(8,128)(2,1)} %bitcast.7, f32[1,256]{1,0:T(1,128)} %bitcast.9, f32[1,256]{1,0:T(1,128)} %bitcast.10), custom_call_target="tpu_custom_call" | custom-call | tf_op jit(solution)/shard_map/section/pallas_call | solution.py:642
  84.5 3.0 %put.1 = (f32[27,256,256]{2,1,0:T(8,128)}, f32[1,256]{1,0:T(1,128)}, f32[1,256]{1,0:T(1,128)}) custom-call(f32[27,256,256]{2,1,0:T(8,128)S(1)} %get-tuple-element.9.gw_ref, f32[1,256]{1,0:T(1,128)S(1)} %get-tuple-element.10.bias_ref, f32[1,256]{1,0:T(1,128)S(1)} %get-tuple-element.11.head_ref), custom_call_target="tpu_custom_call" | custom-call | tf_op jit(solution)/shard_map/put/pallas_call | solution.py:653

commit v5 on v4

--- a/solution.py
+++ b/solution.py
@@ -187,7 +187,7 @@
                     copy.wait_recv()
 
     always = tm >= 0
-    first = ((always, always, same), (has_next, has_prev, nxt), (has_prev, has_next, prv))
+    first = ((has_next, has_prev, nxt[::-1]), (has_prev, has_next, prv[::-1]), (always, always, same))
     exchange(first)
     bias_in.wait()
     head_in.wait()
@@ -334,7 +334,7 @@
                         out[b * 3 + d, fi, :, c * 128:(c + 1) * 128] = rows3[b].astype(BF16)
             return 0
 
-        lax.fori_loop(0, 6, body, 0)
+        lax.fori_loop(0, 6, body, 0, unroll=2)
 
     def correlate(left, right):
         def body(t, _):

time: 87.6 us -> 88 us (level)
  no operation moved by 1% of the time
where the time goes in v5:
time: 88 us; the launch traced here: 87.9 us
  Pallas kernels  87.3 us (99%)
    pallas_call x1, Pallas kernels, per_device(): pl.pallas_call(kernel, out_shape=(pltpu.VMEM((27, C, C), F32), pltpu.VMEM...  84.3 us
    pallas_call x1, Pallas kernels, per_device(): pl.pallas_call(put, out_shape=(jax.ShapeDtypeStruct((27, C, C), F32), jax...  3.01 us

profile of v5, /device:TPU:1, one launch (start us, length us, event | category | flops | bytes accessed | tf_op | source)
XLA Modules:
  0.0 87.9 jit_solution(16463221876331323006)
XLA Ops:
  0.6 84.3 %section.1 = (f32[27,256,256]{2,1,0:T(8,128)S(1)}, f32[1,256]{1,0:T(1,128)S(1)}, f32[1,256]{1,0:T(1,128)S(1)}) custom-call(bf16[2,128,256]{2,1,0:T(8,128)(2,1)} %bitcast.8, bf16[9,768,256]{2,1,0:T(8,128)(2,1)} %bitcast.7, f32[1,256]{1,0:T(1,128)} %bitcast.9, f32[1,256]{1,0:T(1,128)} %bitcast.10), custom_call_target="tpu_custom_call" | custom-call | tf_op jit(solution)/shard_map/section/pallas_call | solution.py:642
  84.9 3.0 %put.1 = (f32[27,256,256]{2,1,0:T(8,128)}, f32[1,256]{1,0:T(1,128)}, f32[1,256]{1,0:T(1,128)}) custom-call(f32[27,256,256]{2,1,0:T(8,128)S(1)} %get-tuple-element.9.gw_ref, f32[1,256]{1,0:T(1,128)S(1)} %get-tuple-element.10.bias_ref, f32[1,256]{1,0:T(1,128)S(1)} %get-tuple-element.11.head_ref), custom_call_target="tpu_custom_call" | custom-call | tf_op jit(solution)/shard_map/put/pallas_call | solution.py:653
